TPU v7x, 256 devices: a whole 4x4x8 slice. The times are simulated.
256 devices in a mesh: seq: 8 (over z), tensor: 8 (over x, y_hi), dp: 4 (over y_lo, core).
Axes of the slice: x: 4, y: 4 (y_hi: 2, y_lo: 2; y = y_hi * 2 + y_lo), z: 8, core: 2. Of those that a mesh axis runs over, the one named last changes fastest.
Arguments:
- tokens: bfloat16 [4, 2048, 3072], P('dp', 'seq'), may hold values from -6 to 6
- cotangent: bfloat16 [4, 2048, 3072], P('dp', 'seq'), may hold values from -6 to 6
- qkv_weight: bfloat16 [3072, 3, 3072], P(('seq', 'dp'), None, 'tensor'), may hold values from -0.109375 to 0.109375
- out_weight: bfloat16 [3072, 3072], P(('seq', 'dp'), 'tensor'), may hold values from -0.109375 to 0.109375
Outputs:
- qkv_grad: float32 [3072, 3, 3072], P(('seq', 'dp'), None, 'tensor')
- out_grad: float32 [3072, 3072], P(('seq', 'dp'), 'tensor')
- branch_grad: bfloat16 [4, 2048, 3072], P('dp', 'seq', 'tensor')
All inputs are finite; a program needn't handle non-finite values.
Results may differ from a plain program's by a relative error of at most 0.025.
Values may be sent and summed in bfloat16 or wider, within the bound.
A program may use at most 128 MiB of HBM per device.

v0:
```python
import jax
import jax.numpy as jnp
from jax import lax
from jax.sharding import PartitionSpec as P

HD = 128


epsilon = 1e-06


def sent_together(arrays, axis, dim, along):
    both = jnp.concatenate(arrays, axis=along)
    result, at, done = (lax.all_gather(both, axis, axis=dim, tiled=True), 0, [])
    for a in arrays:
        done.append(lax.slice_in_dim(result, at, at + a.shape[along], axis=along))
        at += a.shape[along]
    return tuple(done)


def split_up(shard, dim, size):
    before, after = (shard.shape[:dim], shard.shape[dim + 1 :])
    return jnp.moveaxis(shard.reshape(*before, size, -1, *after), dim, 0)


def summed_on_arrival(shard, axis, dim):
    size = lax.axis_size(axis)
    pieces = lax.all_to_all(split_up(shard, dim, size), axis, 0, 0, tiled=True)
    return jnp.sum(pieces.astype(jnp.float32), axis=0)


def copy_for_each(shard, axis):
    copies = jnp.broadcast_to(shard, (lax.axis_size(axis), *shard.shape))
    return lax.all_to_all(copies, axis, split_axis=0, concat_axis=0, tiled=True)


def taken_together(shard, axis):
    everything = copy_for_each(shard, axis)
    return jnp.sum(everything, axis=0)


def in_one(arrays, axis):
    ends = [0]
    for a in arrays:
        ends.append(ends[-1] + a.size)
    subtotal = taken_together(jnp.concatenate([a.ravel() for a in arrays]), axis)
    return tuple((subtotal[b:e].reshape(a.shape) for a, b, e in zip(arrays, ends, ends[1:])))


def normalize(values):
    average = jnp.mean(values, axis=-1, keepdims=True)
    centered = values - average
    inverse = lax.rsqrt(jnp.mean(centered * centered, axis=-1, keepdims=True) + epsilon)
    return (centered * inverse, inverse)


def normalize_back(gradient, normed, inverse):
    mean_grad = jnp.mean(gradient, axis=-1, keepdims=True)
    mean_both = jnp.mean(gradient * normed, axis=-1, keepdims=True)
    return (gradient - mean_grad - normed * mean_both) * inverse


def local(tokens, cotangent, qkv_weight, out_weight):
    row_count = tokens.shape[1]
    feature_count = tokens.shape[2]
    column_count = out_weight.shape[1]
    head_count = column_count // HD
    score_scale = HD ** (-0.5)
    own_rows = qkv_weight.shape[0]
    grad_rows = cotangent[0]
    normed, inverse = normalize(tokens[0].astype(jnp.float32))
    unit_low = normed.astype(jnp.bfloat16)
    flat_weight = qkv_weight.reshape(own_rows, 3 * column_count)
    piece_qkv, piece_out = sent_together((flat_weight, out_weight), ("seq", "dp"), 0, 1)
    piece_rows = piece_qkv.shape[0]
    left_rows = unit_low
    right_rows = grad_rows
    projected = jnp.dot(left_rows, piece_qkv, preferred_element_type=jnp.float32)
    attended_grad = jnp.dot(right_rows, piece_out, preferred_element_type=jnp.float32)
    full_qkv = piece_qkv
    projected, attended_grad, full_qkv = (projected, attended_grad, full_qkv)
    query_unit, query_inv = normalize(
        projected[:, :column_count].reshape(row_count, head_count, HD)
    )
    key_unit, key_inv = normalize(
        projected[:, column_count : 2 * column_count].reshape(row_count, head_count, HD)
    )
    query_low = query_unit.astype(jnp.bfloat16)
    key_value = jnp.stack(
        [
            key_unit.astype(jnp.bfloat16).reshape(row_count, column_count),
            projected[:, 2 * column_count :].astype(jnp.bfloat16),
        ]
    )
    grad_low = attended_grad.astype(jnp.bfloat16).reshape(row_count, head_count, HD)

    def scores_of(key_rows):
        piece_rows = key_rows.shape[0]
        return (
            jnp.einsum(
                "qhd,khd->hqk",
                query_low,
                key_rows.reshape(piece_rows, head_count, HD),
                preferred_element_type=jnp.float32,
            )
            * score_scale
        )

    every_pair = lax.all_gather(key_value, "seq", axis=1, tiled=True)
    piece_rows = every_pair.shape[1]
    exponent = jnp.exp(scores_of(every_pair[0]))
    add_exp_total = jnp.sum(exponent, axis=-1)
    weighted = jnp.einsum(
        "hqk,khd->qhd",
        exponent.astype(jnp.bfloat16),
        every_pair[1].reshape(piece_rows, head_count, HD),
        preferred_element_type=jnp.float32,
    )
    exp_total, weighted = (add_exp_total, weighted)
    attended_low = (weighted / exp_total.T[:, :, None]).astype(jnp.bfloat16)
    row_delta = jnp.sum(grad_low.astype(jnp.float32) * attended_low.astype(jnp.float32), axis=-1)
    piece_rows = every_pair.shape[1]
    key_rows = every_pair[0].reshape(piece_rows, head_count, HD)
    value_rows = every_pair[1].reshape(piece_rows, head_count, HD)
    probability = jnp.exp(scores_of(every_pair[0])) / exp_total[:, :, None]
    prob_grad = jnp.einsum("qhd,khd->hqk", grad_low, value_rows, preferred_element_type=jnp.float32)
    grad_score = (probability * (prob_grad - row_delta.T[:, :, None]) * score_scale).astype(
        jnp.bfloat16
    )
    query_part = jnp.einsum(
        "hqk,khd->qhd", grad_score, key_rows, preferred_element_type=jnp.float32
    )
    key_part = jnp.einsum("hqk,qhd->khd", grad_score, query_low, preferred_element_type=jnp.float32)
    value_part = jnp.einsum(
        "hqk,qhd->khd",
        probability.astype(jnp.bfloat16),
        grad_low,
        preferred_element_type=jnp.float32,
    )
    every_grad = jnp.stack(
        [key_part.reshape(piece_rows, column_count), value_part.reshape(piece_rows, column_count)]
    )
    pair_grad = lax.psum_scatter(
        every_grad.astype(jnp.bfloat16), "seq", scatter_dimension=1, tiled=True
    ).astype(jnp.float32)
    query_back = normalize_back(query_part, query_unit, query_inv)
    key_back = normalize_back(pair_grad[0].reshape(row_count, head_count, HD), key_unit, key_inv)
    qkv_low = jnp.concatenate(
        [
            query_back.reshape(row_count, column_count),
            key_back.reshape(row_count, column_count),
            pair_grad[1],
        ],
        axis=1,
    ).astype(jnp.bfloat16)
    inner_grad = jnp.einsum("rc,dc->rd", qkv_low, full_qkv, preferred_element_type=jnp.float32)
    attended_flat = attended_low.reshape(row_count, column_count)
    share_width = feature_count // lax.axis_size("tensor")
    own_share = summed_on_arrival(inner_grad.astype(jnp.bfloat16), "tensor", 1)
    offset = lax.axis_index("tensor") * share_width
    unit_own = lax.dynamic_slice_in_dim(normed, offset, share_width, 1)
    row_sums = in_one(
        (
            jnp.sum(own_share, axis=1, keepdims=True),
            jnp.sum(own_share * unit_own, axis=1, keepdims=True),
        ),
        "tensor",
    )
    branch = (
        own_share - row_sums[0] / feature_count - unit_own * (row_sums[1] / feature_count)
    ) * inverse
    left_rows = unit_low
    right_rows = grad_rows
    qkv_term = jnp.einsum(
        "rd,rc->dc", left_rows, qkv_low, preferred_element_type=jnp.float32
    ).reshape(lax.axis_size(("seq", "dp")) * own_rows, 3, column_count)
    out_term = jnp.einsum(
        "rd,rc->dc", right_rows, attended_flat, preferred_element_type=jnp.float32
    )
    summed = lax.psum_scatter(
        jnp.concatenate([qkv_term, out_term[:, None, :]], axis=1).astype(jnp.bfloat16),
        ("seq", "dp"),
        scatter_dimension=0,
        tiled=True,
    ).astype(jnp.float32)
    return (summed[:, :3], summed[:, 3], branch.astype(jnp.bfloat16)[None])


def solution(mesh):
    return jax.shard_map(
        local,
        mesh=mesh,
        in_specs=(
            P("dp", "seq", None),
            P("dp", "seq", None),
            P(("seq", "dp"), None, "tensor"),
            P(("seq", "dp"), "tensor"),
        ),
        out_specs=(
            P(("seq", "dp"), None, "tensor"),
            P(("seq", "dp"), "tensor"),
            P("dp", "seq", "tensor"),
        ),
        check_vma=False,
    )
```

profile of v0, /device:TPU:2, one launch (start us, length us, event | category | flops | bytes accessed | tf_op | source)
XLA Modules:
  0.0 412.9 jit_solution(13253095489150140398)
XLA Ops:
  12.4 73.3 %all-gather.3.cloned.1.call-done = bf16[3072,1536]{1,0:T(8,128)(2,1)} async-done(((bf16[96,1536]{1,0:T(8,128)(2,1)}), bf16[3072,1536]{1,0:T(8,128)(2,1)}) %all-gather.3.cloned.1.call-update) | async-done | bytes 9437200 | tf_op jit(solution)/shard_map/all_gather | solution.py:14
  85.7 5.3 %fusion.2 = f32[256,1152]{1,0:T(8,128)S(1)} fusion(bf16[3072,1536]{1,0:T(8,128)(2,1)} %all-gather.3.cloned.1.call-done, bf16[1,256,3072]{2,1,0:T(8,128)(2,1)S(1)} %copy-done.1, f32[256]{0:T(256)S(1)} %add_rsqrt_fusion.2, f32[256]{0:T(256)S(1)} %broadcast_multiply_fusion.6), kind=kOutput, calls=%fused_computation.5 | convolution fusion | flops 1815085056 | bytes 9832448 | tf_op jit(solution)/shard_map/dot_general | solution.py:78
  94.9 1.9 copy.92
  97.6 1.9 copy.91
  99.5 2.2 fusion.65
  104.8 3.2 fusion.38
  108.0 40.1 %all-gather.5.cloned.1.call-done = bf16[2,2048,384]{2,1,0:T(8,128)(2,1)} async-done(((bf16[2,256,384]{2,1,0:T(8,128)(2,1)}), bf16[2,2048,384]{2,1,0:T(8,128)(2,1)}) %all-gather.5.cloned.1.call-update) | async-done | bytes 3145744 | tf_op jit(solution)/shard_map/all_gather | solution.py:109
  148.0 3.9 fusion.64
  152.0 2.6 copy.93
  154.6 2.6 copy.97
  157.2 2.8 fusion.6
  160.0 2.6 fusion.22
  164.4 2.5 multiply_convert_fusion
  170.3 2.6 copy.100
  172.9 2.6 copy.101
  175.5 3.9 pad_maximum_fusion.1
  179.7 3.6 fusion.63
  185.8 3.4 fusion.7
  189.2 36.1 %reduce-scatter.3.cloned.1.call-done = bf16[2,256,384]{2,1,0:T(8,128)(2,1)} async-done(((bf16[2,2048,384]{2,1,0:T(8,128)(2,1)}), bf16[2,256,384]{2,1,0:T(8,128)(2,1)}) %reduce-scatter.3.cloned.1.call-update) | async-done | bytes 393232 | tf_op jit(solution)/shard_map/reduce_scatter | solution.py:143
  225.3 1.9 slice_convert_fusion.1
  227.1 1.9 copy.102
  232.9 1.9 copy.104
  237.0 1.9 fusion.53
  238.9 2.1 copy.107
  241.0 5.7 %convolution_convert_fusion = bf16[3072,3,384]{2,0,1:T(8,128)(2,1)} fusion(bf16[3,384,256]{2,1,0:T(8,128)(2,1)} %bitcast.114, bf16[1,256,3072]{2,1,0:T(8,128)(2,1)S(1)} %copy-done.1, f32[256]{0:T(256)S(1)} %copy-done.14, f32[256]{0:T(256)S(1)} %copy-done.12), kind=kOutput, calls=%fused_computation.7 | convolution fusion | flops 1818624000 | bytes 9242624 | tf_op jit(solution)/shard_map/rd,rc->dc/dot_general | solution.py:174
  246.7 8.4 %pad_maximum_fusion = bf16[3072,4,384]{2,0,1:T(8,128)(2,1)} fusion(bf16[3072,1,384]{2,0,1:T(8,128)(2,1)} %fusion.7, bf16[3072,3,384]{2,0,1:T(8,128)(2,1)} %convolution_convert_fusion), kind=kLoop, calls=%fused_computation | loop fusion | flops 4718592 | bytes 18874368 | tf_op jit(solution)/shard_map/concatenate | solution.py:181
  256.2 5.3 %fusion.8 = bf16[256,3072]{1,0:T(8,128)(2,1)S(1)} fusion(bf16[3072,1536]{1,0:T(8,128)(2,1)} %all-gather.3.cloned.1.call-done, bf16[256,384]{1,0:T(8,128)(2,1)} %get-tuple-element.14, bf16[256,384]{1,0:T(8,128)(2,1)S(1)} %copy-done.8, bf16[256,384]{1,0:T(8,128)(2,1)S(1)} %copy-done.9), kind=kOutput, calls=%fused_computation.18 | convolution fusion | flops 1814495232 | bytes 9240576 | tf_op jit(solution)/shard_map/rc,dc->rd/dot_general | solution.py:156
  262.9 7.3 %all-to-all-start = ((bf16[8,256,384]{2,1,0:T(8,128)(2,1)}), bf16[8,256,384]{2,1,0:T(8,128)(2,1)}, u32[]{:S(2)}, u32[]{:S(2)}) async-start(bf16[8,256,384]{2,1,0:T(8,128)(2,1)} %bitcast.107), calls=%async_computation.2 | async-start | bytes 3145728 | tf_op jit(solution)/shard_map/all_to_all | solution.py:28
  270.1 2.3 fusion.14
  272.4 20.8 %all-to-all-done = bf16[8,256,384]{2,1,0:T(8,128)(2,1)} async-done(((bf16[8,256,384]{2,1,0:T(8,128)(2,1)}), bf16[8,256,384]{2,1,0:T(8,128)(2,1)}, u32[]{:S(2)}, u32[]{:S(2)}) %all-to-all-start) | async-done | bytes 1572896 | tf_op jit(solution)/shard_map/all_to_all | solution.py:28
  296.1 10.3 %all_to_all.11 = f32[8,1,512]{2,1,0:T(1,128)S(1)} all-to-all(f32[8,1,512]{2,1,0:T(1,128)S(1)} %broadcast_in_dim.8), channel_id=1, replica_groups=mesh['seq'=8,'tensor'=8,'dp'=4] {'tensor'}, dimensions={0} | all-to-all | bytes 32768 | tf_op jit(solution)/shard_map/all_to_all | solution.py:34
  308.3 94.6 %reduce-scatter.5.cloned.1.call-done = bf16[96,4,384]{2,0,1:T(8,128)(2,1)} async-done(((bf16[3072,4,384]{2,0,1:T(8,128)(2,1)}), bf16[96,4,384]{2,0,1:T(8,128)(2,1)}) %reduce-scatter.5.cloned.1.call-update) | async-done | bytes 294928 | tf_op jit(solution)/shard_map/reduce_scatter | solution.py:180
  (81 shorter events, 37.5 us)
Async XLA Ops:
  7.2 97.7 %copy-start = (bf16[1,256,3072]{2,1,0:T(8,128)(2,1)S(1)}, bf16[1,256,3072]{2,1,0:T(8,128)(2,1)}, u32[]{:S(2)}) copy-start(bf16[1,256,3072]{2,1,0:T(8,128)(2,1)} %param.5) | copy-start | bytes 4718596
  7.2 4.6 %copy-start.1 = (bf16[1,256,3072]{2,1,0:T(8,128)(2,1)S(1)}, bf16[1,256,3072]{2,1,0:T(8,128)(2,1)}, u32[]{:S(2)}) copy-start(bf16[1,256,3072]{2,1,0:T(8,128)(2,1)} %param.4) | copy-start | bytes 4718596
  7.2 78.5 %all-gather.3.cloned.1.call-start = ((), (), s32[]{:S(2)}) async-start(), calls=%async_computation.4 | async-start | bytes 9732096 | tf_op jit(solution)/shard_map/all_gather | solution.py:14
  10.0 138.1 %all-gather.5.cloned.1.call-start = ((), (), s32[]{:S(2)}) async-start(), calls=%async_computation.5 | async-start | bytes 3538944 | tf_op jit(solution)/shard_map/all_gather | solution.py:109
  11.8 79.2 %copy-start.11 = (f32[256]{0:T(256)}, f32[256]{0:T(256)S(1)}, u32[]{:S(2)}) copy-start(f32[256]{0:T(256)S(1)} %broadcast_multiply_fusion.6) | copy-start | bytes 3076
  12.3 78.6 %copy-start.13 = (f32[256]{0:T(256)}, f32[256]{0:T(256)S(1)}, u32[]{:S(2)}) copy-start(f32[256]{0:T(256)S(1)} %add_rsqrt_fusion.2) | copy-start | bytes 3076
  90.9 1.2 copy-start.6
  94.0 9.5 %copy-start.4 = (f32[256,384]{0,1:T(8,128)}, f32[256,384]{0,1:T(8,128)S(1)}, u32[]{:S(2)}) copy-start(f32[256,384]{0,1:T(8,128)S(1)} %copy.90) | copy-start | bytes 1179652
  103.5 121.8 %reduce-scatter.3.cloned.1.call-start = ((), (), s32[]{:S(2)}) async-start(), calls=%async_computation.6 | async-start | bytes 3538944 | tf_op jit(solution)/shard_map/reduce_scatter | solution.py:143
  157.2 2.8 copy-start.10
  160.0 2.6 copy-start.3
  166.9 1.6 copy-start.2
  179.4 223.5 %reduce-scatter.5.cloned.1.call-start = ((), (), s32[]{:S(2)}) async-start(), calls=%async_computation.7 | async-start | bytes 9732096 | tf_op jit(solution)/shard_map/reduce_scatter | solution.py:180
  184.0 45.0 %copy-start.5 = (f32[256,384]{0,1:T(8,128)S(1)}, f32[256,384]{0,1:T(8,128)}, u32[]{:S(2)}) copy-start(f32[256,384]{0,1:T(8,128)} %copy-done.4) | copy-start | bytes 1179652
  232.1 8.9 %copy-start.12 = (f32[256]{0:T(256)S(1)}, f32[256]{0:T(256)}, u32[]{:S(2)}) copy-start(f32[256]{0:T(256)} %copy-done.11) | copy-start | bytes 3076
  232.1 8.9 %copy-start.14 = (f32[256]{0:T(256)S(1)}, f32[256]{0:T(256)}, u32[]{:S(2)}) copy-start(f32[256]{0:T(256)} %copy-done.13) | copy-start | bytes 3076
  236.4 0.7 copy-start.7
  255.2 0.9 copy-start.8
  255.2 1.0 copy-start.9
  262.9 30.3 %all-to-all-start = ((bf16[8,256,384]{2,1,0:T(8,128)(2,1)}), bf16[8,256,384]{2,1,0:T(8,128)(2,1)}, u32[]{:S(2)}, u32[]{:S(2)}) async-start(bf16[8,256,384]{2,1,0:T(8,128)(2,1)} %bitcast.107), calls=%async_computation.2 | async-start | bytes 3145728 | tf_op jit(solution)/shard_map/all_to_all | solution.py:28
Sparse Core Ops, SparseCore 0:
  10.4 75.1 all-gather.2
  103.6 44.4 all-gather.4
  179.6 45.6 reduce-scatter.2
  255.3 147.5 reduce-scatter.4
where the time goes:
time: 415 us; the launch traced here: 413 us
  waiting for transfers between devices  265 us (64%)
  local copies, waits for them, and re-layouts  42.5 us (10%)
  matrix products  37.9 us (9%)
  other arithmetic  35.6 us (9%)
  between operations  14 us (3%)
  blocking collectives  10.3 us (2%)
  starting transfers between devices  7.6 us (2%)
    reduce_scatter x1, waiting for transfers between devices, local(): lax.psum_scatter(jnp.concatenate([qkv_term, out_term[:, None, :]], axis=1...  94.6 us
    all_gather x1, waiting for transfers between devices, sent_together(): result, at, done = (lax.all_gather(both, axis, axis=dim, tiled=True), 0, [])  73.3 us
    all_gather x1, waiting for transfers between devices, local(): every_pair = lax.all_gather(key_value, 'seq', axis=1, tiled=True)  40.1 us
    reduce_scatter x1, waiting for transfers between devices, local(): lax.psum_scatter(every_grad.astype(jnp.bfloat16), 'seq', scatter_dimensio...  36.1 us
    all_to_all x1, waiting for transfers between devices, summed_on_arrival(): pieces = lax.all_to_all(split_up(shard, dim, size), axis, 0, 0, tiled=True)  20.8 us
    all_to_all x1, blocking collectives, copy_for_each(): return lax.all_to_all(copies, axis, split_axis=0, concat_axis=0, tiled=True)  10.3 us
    concatenate x1, other arithmetic, local(): jnp.concatenate([qkv_term, out_term[:, None, :]], axis=1)  8.45 us
  transfers between devices with their start and end apart: 5, of which 5 were waited for; matrix products, arithmetic and copies ran while one was open for 7% of the time, Pallas kernels for 0%

commit v1 on v0

--- a/solution.py
+++ b/solution.py
@@ -1,9 +1,14 @@
 import jax
 import jax.numpy as jnp
 from jax import lax
+from jax.experimental import pallas as pl
+from jax.experimental.pallas import tpu as pltpu
 from jax.sharding import PartitionSpec as P
 
 HD = 128
+MESH = pl.DeviceIdType.MESH
+F32 = jnp.float32
+BF16 = jnp.bfloat16
 
 
 epsilon = 1e-06
@@ -60,12 +65,248 @@
     return (gradient - mean_grad - normed * mean_both) * inverse
 
 
+NZ = 8
+
+
+def twice(a):
+    return jnp.concatenate([a, a], axis=1)
+
+
+def lane_mean(a):
+    return jnp.broadcast_to(jnp.mean(a, axis=1, keepdims=True), a.shape)
+
+
+def attention_kernel(
+    heads,
+    proj,
+    grad,
+    qkv_out,
+    att_out,
+    q_low,
+    do,
+    unit,
+    inv,
+    kv,
+    ex,
+    dp,
+    wsum,
+    tsum,
+    rtot,
+    delta,
+    dq,
+    part,
+    sbuf,
+    rbuf,
+    send_ag,
+    recv_ag,
+    send_rs,
+    recv_rs,
+):
+    me = lax.axis_index("seq")
+    sides = (lax.rem(me + 1, NZ), lax.rem(me + NZ - 1, NZ))
+    scale = HD ** (-0.5)
+    width = heads * HD
+
+    barrier = pltpu.get_barrier_semaphore()
+    for side in sides:
+        pl.semaphore_signal(barrier, inc=1, device_id={"seq": side}, device_id_type=MESH)
+
+    for h in range(heads):
+        for j in range(2):
+            a = proj[:, (j * heads + h) * HD : (j * heads + h + 1) * HD]
+            c = a - lane_mean(a)
+            r = lax.rsqrt(lane_mean(c * c) + epsilon)
+            u = c * r
+            unit[j, h] = u
+            inv[j, h] = r
+            if j == 0:
+                q_low[h] = u.astype(BF16)
+            else:
+                kv[me, 0, h] = u.astype(BF16)
+        kv[me, 1, h] = proj[:, (2 * heads + h) * HD : (2 * heads + h + 1) * HD].astype(BF16)
+        do[h] = grad[:, h * HD : (h + 1) * HD]
+        wsum[h] = jnp.zeros_like(wsum[h])
+        tsum[h] = jnp.zeros_like(tsum[h])
+        dq[h] = jnp.zeros_like(dq[h])
+
+    pl.semaphore_wait(barrier, 2)
+
+    def gather(way, step, j):
+        b = lax.rem(me + (NZ - step if way == 0 else step), NZ)
+        return pltpu.make_async_remote_copy(
+            src_ref=kv.at[b, j],
+            dst_ref=kv.at[b, j],
+            send_sem=send_ag.at[way, step, j],
+            recv_sem=recv_ag.at[way, step, j],
+            device_id={"seq": sides[way]},
+            device_id_type=MESH,
+        )
+
+    def scatter(way, step, j):
+        return pltpu.make_async_remote_copy(
+            src_ref=sbuf.at[way, step, j],
+            dst_ref=rbuf.at[way, step, j],
+            send_sem=send_rs.at[way, step, j],
+            recv_sem=recv_rs.at[way, step, j],
+            device_id={"seq": sides[way]},
+            device_id_type=MESH,
+        )
+
+    def goes(way, step, j):
+        return step < 3 or j == way
+
+    def forward(b, h):
+        k = kv[b, 0, h]
+        v = kv[b, 1, h]
+        s = lax.dot_general(q_low[h], k, (((1,), (1,)), ((), ())), preferred_element_type=F32)
+        e = jnp.exp(s * scale)
+        ex[b, h] = e
+        tsum[h] = tsum[h] + (e[:, :HD] + e[:, HD:])
+        wsum[h] = wsum[h] + jnp.dot(e.astype(BF16), v, preferred_element_type=F32)
+        dp[b, h] = lax.dot_general(
+            do[h], v, (((1,), (1,)), ((), ())), preferred_element_type=F32
+        )
+
+    def forward_blocks(ahead, behind):
+        def step(i, c):
+            way = i // heads
+            b = lax.rem(me + ahead + way * (behind - ahead), NZ)
+            forward(b, lax.rem(i, heads))
+            return c
+
+        n = heads if ahead == behind else 2 * heads
+        lax.fori_loop(0, n, step, 0)
+
+    for j in range(2):
+        for way in range(2):
+            gather(way, 0, j).start()
+    forward_blocks(0, 0)
+    for step in range(3):
+        for j in range(2):
+            for way in range(2):
+                gather(way, step, j).wait_recv()
+                if goes(way, step + 1, j):
+                    gather(way, step + 1, j).start()
+        forward_blocks(NZ - 1 - step, 1 + step)
+    gather(0, 3, 0).wait_recv()
+    gather(1, 3, 1).wait_recv()
+    forward_blocks(4, 4)
+
+    for h in range(heads):
+        total = jnp.broadcast_to(jnp.sum(tsum[h], axis=1, keepdims=True), tsum[h].shape)
+        low = (wsum[h] / total).astype(BF16)
+        att_out[:, h * HD : (h + 1) * HD] = low
+        rtot[h] = 1.0 / total
+        g = do[h].astype(F32) * low.astype(F32)
+        delta[h] = jnp.broadcast_to(jnp.sum(g, axis=1, keepdims=True), g.shape)
+
+    def backward(b, h, slot):
+        p = ex[b, h] * twice(rtot[h])
+        ds = (p * (dp[b, h] - twice(delta[h])) * scale).astype(BF16)
+        dq[h] = dq[h] + jnp.dot(ds, kv[b, 0, h], preferred_element_type=F32)
+        part[slot, 0, h] = lax.dot_general(
+            ds, q_low[h], (((0,), (0,)), ((), ())), preferred_element_type=F32
+        )
+        part[slot, 1, h] = lax.dot_general(
+            p.astype(BF16), do[h], (((0,), (0,)), ((), ())), preferred_element_type=F32
+        )
+
+    def backward_blocks(ahead, behind):
+        def step(i, c):
+            way = i // heads
+            b = lax.rem(me + ahead + way * (behind - ahead), NZ)
+            backward(b, lax.rem(i, heads), way)
+            return c
+
+        n = heads if ahead == behind else 2 * heads
+        lax.fori_loop(0, n, step, 0)
+
+    for step in range(4):
+        ahead, behind = 4 - step, 4 + step
+        backward_blocks(ahead, behind)
+        for j in range(2):
+            for way in range(2):
+                if not goes(way, 3 - step, j):
+                    continue
+                slot = 0 if step == 0 else way
+                if step > 0 and goes(way, 4 - step, j):
+                    scatter(way, step - 1, j).wait_recv()
+                    sbuf[way, step, j] = (
+                        part[slot, j] + rbuf[way, step - 1, j].astype(F32)
+                    ).astype(BF16)
+                else:
+                    sbuf[way, step, j] = part[slot, j].astype(BF16)
+                scatter(way, step, j).start()
+    backward_blocks(0, 0)
+
+    def back(g, j, h):
+        u = unit[j, h]
+        return (g - lane_mean(g) - u * lane_mean(g * u)) * inv[j, h]
+
+    for h in range(heads):
+        qkv_out[:, h * HD : (h + 1) * HD] = back(dq[h], 0, h).astype(BF16)
+    for j in range(2):
+        for way in range(2):
+            scatter(way, 3, j).wait_recv()
+        for h in range(heads):
+            g = part[0, j, h] + rbuf[0, 3, j, h].astype(F32) + rbuf[1, 3, j, h].astype(F32)
+            if j == 0:
+                g = back(g, 1, h)
+            at = (j + 1) * width + h * HD
+            qkv_out[:, at : at + HD] = g.astype(BF16)
+    for step in range(4):
+        for j in range(2):
+            for way in range(2):
+                if goes(way, step, j):
+                    gather(way, step, j).wait_send()
+                if goes(way, 3 - step, j):
+                    scatter(way, step, j).wait_send()
+
+
+def attention(proj, grad):
+    rows = proj.shape[0]
+    heads = grad.shape[1] // HD
+    vmem = pl.BlockSpec(memory_space=pltpu.VMEM)
+    one = (heads, rows, HD)
+    return pl.pallas_call(
+        lambda *refs: attention_kernel(heads, *refs),
+        out_shape=(
+            jax.ShapeDtypeStruct(proj.shape, BF16),
+            jax.ShapeDtypeStruct(grad.shape, BF16),
+        ),
+        in_specs=[vmem, vmem],
+        out_specs=(vmem, vmem),
+        scratch_shapes=[
+            pltpu.VMEM(one, BF16),
+            pltpu.VMEM(one, BF16),
+            pltpu.VMEM((2, *one), F32),
+            pltpu.VMEM((2, *one), F32),
+            pltpu.VMEM((NZ, 2, *one), BF16),
+            pltpu.VMEM((NZ, heads, rows, rows), F32),
+            pltpu.VMEM((NZ, heads, rows, rows), F32),
+            pltpu.VMEM(one, F32),
+            pltpu.VMEM(one, F32),
+            pltpu.VMEM(one, F32),
+            pltpu.VMEM(one, F32),
+            pltpu.VMEM(one, F32),
+            pltpu.VMEM((2, 2, *one), F32),
+            pltpu.VMEM((2, 4, 2, *one), BF16),
+            pltpu.VMEM((2, 4, 2, *one), BF16),
+            pltpu.SemaphoreType.DMA((2, 4, 2)),
+            pltpu.SemaphoreType.DMA((2, 4, 2)),
+            pltpu.SemaphoreType.DMA((2, 4, 2)),
+            pltpu.SemaphoreType.DMA((2, 4, 2)),
+        ],
+        compiler_params=pltpu.CompilerParams(
+            collective_id=0, has_side_effects=True, vmem_limit_bytes=60 * 1024 * 1024
+        ),
+    )(proj, grad)
+
+
 def local(tokens, cotangent, qkv_weight, out_weight):
     row_count = tokens.shape[1]
     feature_count = tokens.shape[2]
     column_count = out_weight.shape[1]
-    head_count = column_count // HD
-    score_scale = HD ** (-0.5)
     own_rows = qkv_weight.shape[0]
     grad_rows = cotangent[0]
     normed, inverse = normalize(tokens[0].astype(jnp.float32))
@@ -79,80 +320,7 @@
     attended_grad = jnp.dot(right_rows, piece_out, preferred_element_type=jnp.float32)
     full_qkv = piece_qkv
     projected, attended_grad, full_qkv = (projected, attended_grad, full_qkv)
-    query_unit, query_inv = normalize(
-        projected[:, :column_count].reshape(row_count, head_count, HD)
-    )
-    key_unit, key_inv = normalize(
-        projected[:, column_count : 2 * column_count].reshape(row_count, head_count, HD)
-    )
-    query_low = query_unit.astype(jnp.bfloat16)
-    key_value = jnp.stack(
-        [
-            key_unit.astype(jnp.bfloat16).reshape(row_count, column_count),
-            projected[:, 2 * column_count :].astype(jnp.bfloat16),
-        ]
-    )
-    grad_low = attended_grad.astype(jnp.bfloat16).reshape(row_count, head_count, HD)
-
-    def scores_of(key_rows):
-        piece_rows = key_rows.shape[0]
-        return (
-            jnp.einsum(
-                "qhd,khd->hqk",
-                query_low,
-                key_rows.reshape(piece_rows, head_count, HD),
-                preferred_element_type=jnp.float32,
-            )
-            * score_scale
-        )
-
-    every_pair = lax.all_gather(key_value, "seq", axis=1, tiled=True)
-    piece_rows = every_pair.shape[1]
-    exponent = jnp.exp(scores_of(every_pair[0]))
-    add_exp_total = jnp.sum(exponent, axis=-1)
-    weighted = jnp.einsum(
-        "hqk,khd->qhd",
-        exponent.astype(jnp.bfloat16),
-        every_pair[1].reshape(piece_rows, head_count, HD),
-        preferred_element_type=jnp.float32,
-    )
-    exp_total, weighted = (add_exp_total, weighted)
-    attended_low = (weighted / exp_total.T[:, :, None]).astype(jnp.bfloat16)
-    row_delta = jnp.sum(grad_low.astype(jnp.float32) * attended_low.astype(jnp.float32), axis=-1)
-    piece_rows = every_pair.shape[1]
-    key_rows = every_pair[0].reshape(piece_rows, head_count, HD)
-    value_rows = every_pair[1].reshape(piece_rows, head_count, HD)
-    probability = jnp.exp(scores_of(every_pair[0])) / exp_total[:, :, None]
-    prob_grad = jnp.einsum("qhd,khd->hqk", grad_low, value_rows, preferred_element_type=jnp.float32)
-    grad_score = (probability * (prob_grad - row_delta.T[:, :, None]) * score_scale).astype(
-        jnp.bfloat16
-    )
-    query_part = jnp.einsum(
-        "hqk,khd->qhd", grad_score, key_rows, preferred_element_type=jnp.float32
-    )
-    key_part = jnp.einsum("hqk,qhd->khd", grad_score, query_low, preferred_element_type=jnp.float32)
-    value_part = jnp.einsum(
-        "hqk,qhd->khd",
-        probability.astype(jnp.bfloat16),
-        grad_low,
-        preferred_element_type=jnp.float32,
-    )
-    every_grad = jnp.stack(
-        [key_part.reshape(piece_rows, column_count), value_part.reshape(piece_rows, column_count)]
-    )
-    pair_grad = lax.psum_scatter(
-        every_grad.astype(jnp.bfloat16), "seq", scatter_dimension=1, tiled=True
-    ).astype(jnp.float32)
-    query_back = normalize_back(query_part, query_unit, query_inv)
-    key_back = normalize_back(pair_grad[0].reshape(row_count, head_count, HD), key_unit, key_inv)
-    qkv_low = jnp.concatenate(
-        [
-            query_back.reshape(row_count, column_count),
-            key_back.reshape(row_count, column_count),
-            pair_grad[1],
-        ],
-        axis=1,
-    ).astype(jnp.bfloat16)
+    qkv_low, attended_low = attention(projected, attended_grad.astype(jnp.bfloat16))
     inner_grad = jnp.einsum("rc,dc->rd", qkv_low, full_qkv, preferred_element_type=jnp.float32)
     attended_flat = attended_low.reshape(row_count, column_count)
     share_width = feature_count // lax.axis_size("tensor")

time: 415 us -> 344 us (0.83)
  waiting for transfers between devices: 265 us -> 187 us
  Pallas kernels: 0 us -> 71.2 us
  local copies, waits for them, and re-layouts: 42.5 us -> 7 us
  other arithmetic: 35.6 us -> 20.5 us
  matrix products: 37.9 us -> 23.1 us
    pallas_call x0 -> x1, Pallas kernels: none -> 71.2 us  [attention(): pl.pallas_call(lambda *refs: attention_kernel(heads, *refs), out_shape=(j...]
    all_gather x1 -> x0, waiting for transfers between devices: 40.1 us -> none  [local(): every_pair = lax.all_gather(key_value, 'seq', axis=1, tiled=True)]
    reduce_scatter x1 -> x0, waiting for transfers between devices: 36.1 us -> none  [local(): lax.psum_scatter(every_grad.astype(jnp.bfloat16), 'seq', scatter_dimensio...]
    dot_general x6 -> x0, matrix products: 15 us -> none  [the longest x1 3.56 us: local(): jnp.einsum('hqk,khd->qhd', grad_score, key_rows, preferred_element_type=j...]
    slice x7 -> x0, local copies, waits for them, and re-layouts: 14.2 us -> none  [the longest x2 6.52 us: local(): key_rows = every_pair[0].reshape(piece_rows, head_count, HD)]
    another operation x4 -> x0, other arithmetic: 7.97 us -> none  [the longest x1 3.9 us: local(): jnp.stack([key_part.reshape(piece_rows, column_count), value_part.reshape...]
    another operation x3 -> x0, local copies, waits for them, and re-layouts: 5.91 us -> none  [the longest x2 5.21 us: local(): jnp.stack([key_part.reshape(piece_rows, column_count), value_part.reshape...]
    mul x4 -> x0, local copies, waits for them, and re-layouts: 5.41 us -> none  [the longest x2 2.72 us: normalize(): return (centered * inverse, inverse)]
  transfers between devices with their start and end apart: 5 -> 3, of which waited for: 5 -> 3; matrix products, arithmetic and copies ran while one was open for 7% -> 5% of each run, Pallas kernels for 0% -> 0%
where the time goes in v1:
time: 344 us; the launch traced here: 342 us
  waiting for transfers between devices  187 us (54%)
  Pallas kernels  71.2 us (21%)
  matrix products  23.1 us (7%)
  other arithmetic  20.5 us (6%)
  between operations  14.1 us (4%)
  blocking collectives  11.5 us (3%)
  starting transfers between devices  7.53 us (2%)
  local copies, waits for them, and re-layouts  7 us (2%)
    reduce_scatter x1, waiting for transfers between devices, local(): lax.psum_scatter(jnp.concatenate([qkv_term, out_term[:, None, :]], axis=1...  93.3 us
    all_gather x1, waiting for transfers between devices, sent_together(): result, at, done = (lax.all_gather(both, axis, axis=dim, tiled=True), 0, [])  73.3 us
    pallas_call x1, Pallas kernels, attention(): pl.pallas_call(lambda *refs: attention_kernel(heads, *refs), out_shape=(j...  71.2 us
    all_to_all x1, waiting for transfers between devices, summed_on_arrival(): pieces = lax.all_to_all(split_up(shard, dim, size), axis, 0, 0, tiled=True)  20.6 us
    all_to_all x1, blocking collectives, copy_for_each(): return lax.all_to_all(copies, axis, split_axis=0, concat_axis=0, tiled=True)  11.5 us
    concatenate x1, other arithmetic, local(): jnp.concatenate([qkv_term, out_term[:, None, :]], axis=1)  8.45 us
    all_to_all x1, starting transfers between devices, summed_on_arrival(): pieces = lax.all_to_all(split_up(shard, dim, size), axis, 0, 0, tiled=True)  7.45 us
  transfers between devices with their start and end apart: 3, of which 3 were waited for; matrix products, arithmetic and copies ran while one was open for 5% of the time, Pallas kernels for 0%

profile of v1, /device:TPU:2, one launch (start us, length us, event | category | flops | bytes accessed | tf_op | source)
XLA Modules:
  0.0 342.2 jit_solution(13774954814893802678)
XLA Ops:
  7.2 0.0 copy-start
  7.2 0.0 copy-start.1
  7.2 0.0 all-gather.2.cloned.1.call-start
  7.2 1.1 copy.43
  8.3 1.6 pad_maximum_fusion.1
  10.0 0.0 all-gather.2.cloned.1.call-update
  10.0 0.0 reduce-scatter.2.cloned.1.call-start
  10.0 1.7 convert_reduce_fusion
  11.8 0.0 copy-done.1
  11.8 0.6 fusion.13
  12.3 73.3 %all-gather.2.cloned.1.call-done = bf16[3072,1536]{1,0:T(8,128)(2,1)} async-done(((bf16[96,1536]{1,0:T(8,128)(2,1)}), bf16[3072,1536]{1,0:T(8,128)(2,1)}) %all-gather.2.cloned.1.call-update) | async-done | bytes 9437200 | tf_op jit(solution)/shard_map/all_gather | solution.py:19
  85.7 3.3 fusion.28.refs_1_
  89.0 6.3 %fusion.2.refs_0_ = f32[256,1152]{1,0:T(8,128)} fusion(bf16[3072,1536]{1,0:T(8,128)(2,1)} %all-gather.2.cloned.1.call-done, bf16[1,256,3072]{2,1,0:T(8,128)(2,1)S(1)} %copy-done.1, f32[256]{0:T(256)S(1)} %add_rsqrt_fusion, f32[256]{0:T(256)S(1)} %broadcast_multiply_fusion), kind=kOutput, calls=%fused_computation.3 | convolution fusion | flops 1815085056 | bytes 9832448 | tf_op jit(solution)/shard_map/dot_general | solution.py:319
  95.3 71.2 %shard_map.67 = (bf16[256,1152]{1,0:T(8,128)(2,1)}, bf16[256,384]{1,0:T(8,128)(2,1)}) custom-call(f32[256,1152]{1,0:T(8,128)} %fusion.2.refs_0_, bf16[256,384]{1,0:T(8,128)(2,1)} %fusion.28.refs_1_), custom_call_target="tpu_custom_call" | custom-call | tf_op jit(solution)/shard_map/pallas_call | solution.py:271
  166.4 2.1 copy.30
  168.6 3.4 %fusion.4 = bf16[3072,1,384]{2,0,1:T(8,128)(2,1)} fusion(bf16[256,384]{1,0:T(8,128)(2,1)} %get-tuple-element.6, bf16[1,256,3072]{2,1,0:T(8,128)(2,1)S(1)} %copy-done), kind=kOutput, calls=%fused_computation.12 | convolution fusion | flops 605159424 | bytes 4128768 | tf_op jit(solution)/shard_map/rd,rc->dc/dot_general | solution.py:345
  172.0 4.6 %convolution_convert_fusion = bf16[3072,3,384]{2,0,1:T(8,128)(2,1)} fusion(bf16[3,384,256]{2,1,0:T(8,128)(2,1)S(1)} %bitcast.52, bf16[1,256,3072]{2,1,0:T(8,128)(2,1)S(1)} %copy-done.1, f32[256]{0:T(256)S(1)} %add_rsqrt_fusion, f32[256]{0:T(256)S(1)} %broadcast_multiply_fusion), kind=kOutput, calls=%fused_computation.5 | convolution fusion | flops 1818624000 | bytes 9242624 | tf_op jit(solution)/shard_map/rd,rc->dc/dot_general | solution.py:342
  176.6 8.4 %pad_maximum_fusion = bf16[3072,4,384]{2,0,1:T(8,128)(2,1)} fusion(bf16[3072,1,384]{2,0,1:T(8,128)(2,1)} %fusion.4, bf16[3072,3,384]{2,0,1:T(8,128)(2,1)} %convolution_convert_fusion), kind=kLoop, calls=%fused_computation | loop fusion | flops 4718592 | bytes 18874368 | tf_op jit(solution)/shard_map/concatenate | solution.py:349
  185.1 0.0 reduce-scatter.2.cloned.1.call-update
  185.1 5.4 %fusion.5 = bf16[256,3072]{1,0:T(8,128)(2,1)S(1)} fusion(bf16[256,1152]{1,0:T(8,128)(2,1)} %get-tuple-element.5, bf16[3072,1536]{1,0:T(8,128)(2,1)} %all-gather.2.cloned.1.call-done), kind=kOutput, calls=%fused_computation.13 | convolution fusion | flops 1812725760 | bytes 9240576 | tf_op jit(solution)/shard_map/rc,dc->rd/dot_general | solution.py:324
  190.6 1.3 copy.45
  191.9 7.5 %all-to-all-start = ((bf16[8,256,384]{2,1,0:T(8,128)(2,1)}), bf16[8,256,384]{2,1,0:T(8,128)(2,1)}, u32[]{:S(2)}, u32[]{:S(2)}) async-start(bf16[8,256,384]{2,1,0:T(8,128)(2,1)} %bitcast.51), calls=%async_computation.1 | async-start | bytes 3145728 | tf_op jit(solution)/shard_map/all_to_all | solution.py:33
  199.4 2.3 fusion.11
  201.6 20.6 %all-to-all-done = bf16[8,256,384]{2,1,0:T(8,128)(2,1)} async-done(((bf16[8,256,384]{2,1,0:T(8,128)(2,1)}), bf16[8,256,384]{2,1,0:T(8,128)(2,1)}, u32[]{:S(2)}, u32[]{:S(2)}) %all-to-all-start) | async-done | bytes 1572896 | tf_op jit(solution)/shard_map/all_to_all | solution.py:33
  222.2 1.8 convert_reduce_fusion.1
  224.1 1.1 multiply_reduce_fusion
  225.2 11.5 %all_to_all.11 = f32[8,1,512]{2,1,0:T(1,128)S(1)} all-to-all(f32[8,1,512]{2,1,0:T(1,128)S(1)} %broadcast_in_dim.13), channel_id=1, replica_groups=mesh['seq'=8,'tensor'=8,'dp'=4] {'tensor'}, dimensions={0} | all-to-all | bytes 32768 | tf_op jit(solution)/shard_map/all_to_all | solution.py:39
  236.8 1.9 fusion.33
  238.6 93.3 %reduce-scatter.2.cloned.1.call-done = bf16[96,4,384]{2,0,1:T(8,128)(2,1)} async-done(((bf16[3072,4,384]{2,0,1:T(8,128)(2,1)}), bf16[96,4,384]{2,0,1:T(8,128)(2,1)}) %reduce-scatter.2.cloned.1.call-update) | async-done | bytes 294928 | tf_op jit(solution)/shard_map/reduce_scatter | solution.py:348
  331.9 1.0 convert_element_type.40
  332.9 0.7 slice_bitcast_fusion
  333.6 1.7 slice.26
  (9 shorter events, 0.1 us)
Async XLA Ops:
  7.2 78.5 %copy-start = (bf16[1,256,3072]{2,1,0:T(8,128)(2,1)S(1)}, bf16[1,256,3072]{2,1,0:T(8,128)(2,1)}, u32[]{:S(2)}) copy-start(bf16[1,256,3072]{2,1,0:T(8,128)(2,1)} %param.5) | copy-start | bytes 4718596
  7.2 4.6 %copy-start.1 = (bf16[1,256,3072]{2,1,0:T(8,128)(2,1)S(1)}, bf16[1,256,3072]{2,1,0:T(8,128)(2,1)}, u32[]{:S(2)}) copy-start(bf16[1,256,3072]{2,1,0:T(8,128)(2,1)} %param.4) | copy-start | bytes 4718596
  7.2 78.5 %all-gather.2.cloned.1.call-start = ((), (), s32[]{:S(2)}) async-start(), calls=%async_computation.3 | async-start | bytes 9732096 | tf_op jit(solution)/shard_map/all_gather | solution.py:19
  10.0 321.9 %reduce-scatter.2.cloned.1.call-start = ((), (), s32[]{:S(2)}) async-start(), calls=%async_computation.4 | async-start | bytes 9732096 | tf_op jit(solution)/shard_map/reduce_scatter | solution.py:348
  168.6 3.5 %copy-start.2 = (bf16[1152,256]{1,0:T(8,128)(2,1)S(1)}, bf16[1152,256]{1,0:T(8,128)(2,1)}, u32[]{:S(2)}) copy-start(bf16[1152,256]{1,0:T(8,128)(2,1)} %copy.30) | copy-start | bytes 1769476
  191.9 30.3 %all-to-all-start = ((bf16[8,256,384]{2,1,0:T(8,128)(2,1)}), bf16[8,256,384]{2,1,0:T(8,128)(2,1)}, u32[]{:S(2)}, u32[]{:S(2)}) async-start(bf16[8,256,384]{2,1,0:T(8,128)(2,1)} %bitcast.51), calls=%async_computation.1 | async-start | bytes 3145728 | tf_op jit(solution)/shard_map/all_to_all | solution.py:33
Sparse Core Ops, SparseCore 0:
  10.4 75.1 all-gather.1
  185.2 146.6 reduce-scatter.1

commit v2 on v1

v2 whole, which is shorter than its diff:
```python
import jax
import jax.numpy as jnp
from jax import lax
from jax.experimental import pallas as pl
from jax.experimental.pallas import tpu as pltpu
from jax.sharding import PartitionSpec as P

HD = 128
NZ = 8
NT = 8
NQ = 4
MESH = pl.DeviceIdType.MESH
F32 = jnp.float32
BF16 = jnp.bfloat16
LAST = (((1,), (1,)), ((), ()))
FIRST = (((0,), (0,)), ((), ()))
epsilon = 1e-06


def dot(a, b, dims=(((1,), (0,)), ((), ()))):
    return lax.dot_general(a, b, dims, preferred_element_type=F32)


def twice(a):
    return jnp.concatenate([a, a], axis=1)


def lane_mean(a):
    return jnp.broadcast_to(jnp.mean(a, axis=1, keepdims=True), a.shape)


def lane_sum(a):
    return jnp.broadcast_to(jnp.sum(a, axis=1, keepdims=True), a.shape)


def layer_kernel(
    heads,
    proj,
    grad,
    inverse,
    normed,
    weight,
    unit_t,
    cot_t,
    dw_out,
    branch_out,
    q_low,
    do,
    unit,
    inv,
    kv,
    ex,
    dp,
    wsum,
    tsum,
    rtot,
    delta,
    dq,
    sbuf,
    rbuf,
    act,
    low,
    ut,
    ct,
    w,
    nb,
    own_unit,
    sdw,
    rdw,
    dwp,
    xs,
    xr,
    ysend,
    yrecv,
    stats,
    send_ag,
    recv_ag,
    send_rs,
    recv_rs,
    send_tr,
    recv_tr,
    send_act,
    recv_act,
    send_dw,
    recv_dw,
    send_x,
    recv_x,
    send_y,
    recv_y,
    send_st,
    recv_st,
    load_w,
    load_n,
    load_t,
):
    me = lax.axis_index("seq")
    quad = lax.axis_index("dp")
    part = lax.axis_index("tensor")
    sides = (lax.rem(me + 1, NZ), lax.rem(me + NZ - 1, NZ))
    mates = (quad + 1 - 2 * lax.rem(quad, 2), lax.rem(quad + 2, NQ), NQ - 1 - quad)
    xsides = (lax.rem(part + 2, NT), lax.rem(part + NT - 2, NT))
    ymate = part + 1 - 2 * lax.rem(part, 2)
    yhalf = lax.rem(part, 2)
    xplace = part // 2
    scale = HD ** (-0.5)
    width = heads * HD
    features = NT * width

    barrier = pltpu.get_barrier_semaphore()
    for side in sides:
        pl.semaphore_signal(barrier, inc=1, device_id={"seq": side}, device_id_type=MESH)
    for mate in mates:
        pl.semaphore_signal(barrier, inc=1, device_id={"dp": mate}, device_id_type=MESH)
    for k in range(1, NT):
        pl.semaphore_signal(
            barrier, inc=1, device_id={"tensor": lax.rem(part + k, NT)}, device_id_type=MESH
        )

    def remote(src, dst, send, recv, where):
        return pltpu.make_async_remote_copy(
            src_ref=src,
            dst_ref=dst,
            send_sem=send,
            recv_sem=recv,
            device_id=where,
            device_id_type=MESH,
        )

    def gather(way, step, j):
        b = lax.rem(me + (NZ - step if way == 0 else step), NZ)
        return remote(
            kv.at[b, j],
            kv.at[b, j],
            send_ag.at[way, step, j],
            recv_ag.at[way, step, j],
            {"seq": sides[way]},
        )

    def scatter(way, step, j):
        return remote(
            sbuf.at[way, step, j],
            rbuf.at[way, step, j],
            send_rs.at[way, step, j],
            recv_rs.at[way, step, j],
            {"seq": sides[way]},
        )

    def weight_ring(way, step, half):
        return remote(
            sdw.at[way, step, half],
            rdw.at[way, step, half],
            send_dw.at[way, step, half],
            recv_dw.at[way, step, half],
            {"seq": sides[way]},
        )

    def transposed(k, which):
        src, dst = ((unit_t, ut), (cot_t, ct))[which]
        return remote(
            src.at[:, mates[k]],
            dst.at[quad],
            send_tr.at[k, which],
            recv_tr.at[k, which],
            {"dp": mates[k]},
        )

    def shared(group, k):
        block = act.at[group, quad if k < 2 else mates[1]]
        return remote(
            block,
            block,
            send_act.at[group, k],
            recv_act.at[group, k],
            {"dp": mates[1] if k == 1 else mates[0]},
        )

    def xring(way, step, half):
        return remote(
            xs.at[way, step, half],
            xr.at[way, step, half],
            send_x.at[way, step, half],
            recv_x.at[way, step, half],
            {"tensor": xsides[way]},
        )

    def ypair():
        return remote(ysend, yrecv, send_y, recv_y, {"tensor": ymate})

    def stat(k):
        return remote(
            stats.at[0],
            stats.at[k],
            send_st.at[k - 1],
            recv_st.at[k - 1],
            {"tensor": lax.rem(part + k, NT)},
        )

    def goes(way, step, j):
        return step < 3 or j == way

    load_weight = pltpu.make_async_copy(weight, w, load_w)
    load_weight.start()
    load_normed = [
        pltpu.make_async_copy(
            normed.at[:, t * width : (t + 1) * width], nb.at[t], load_n.at[t]
        )
        for t in range(NT)
    ]
    load_own = [
        pltpu.make_async_copy(unit_t.at[:, quad], ut.at[quad], load_t.at[0]),
        pltpu.make_async_copy(cot_t.at[:, quad], ct.at[quad], load_t.at[1]),
    ]
    for c in load_normed + load_own:
        c.start()

    for h in range(heads):
        for j in range(2):
            a = proj[:, (j * heads + h) * HD : (j * heads + h + 1) * HD]
            c = a - lane_mean(a)
            r = lax.rsqrt(lane_mean(c * c) + epsilon)
            u = c * r
            unit[j, h] = u
            inv[j, h] = r
            if j == 0:
                q_low[h] = u.astype(BF16)
            else:
                kv[me, 0, h] = u.astype(BF16)
        kv[me, 1, h] = proj[:, (2 * heads + h) * HD : (2 * heads + h + 1) * HD].astype(BF16)
        do[h] = grad[:, h * HD : (h + 1) * HD]
        wsum[h] = jnp.zeros_like(wsum[h])
        tsum[h] = jnp.zeros_like(tsum[h])
        dq[h] = jnp.zeros_like(dq[h])

    pl.semaphore_wait(barrier, 2 + 3 + NT - 1)

    def forward(b, h):
        k = kv[b, 0, h]
        v = kv[b, 1, h]
        e = jnp.exp(dot(q_low[h], k, LAST) * scale)
        ex[b, h] = e
        tsum[h] = tsum[h] + (e[:, :HD] + e[:, HD:])
        wsum[h] = wsum[h] + dot(e.astype(BF16), v)
        dp[b, h] = dot(do[h], v, LAST)

    def forward_blocks(ahead, behind):
        def step(i, c):
            b = lax.rem(me + ahead + (i // heads) * (behind - ahead), NZ)
            forward(b, lax.rem(i, heads))
            return c

        lax.fori_loop(0, heads if ahead == behind else 2 * heads, step, 0)

    for j in range(2):
        for way in range(2):
            gather(way, 0, j).start()
    for which in range(2):
        for k in range(3):
            transposed(k, which).start()
    forward_blocks(0, 0)
    for step in range(3):
        for j in range(2):
            for way in range(2):
                gather(way, step, j).wait_recv()
                if goes(way, step + 1, j):
                    gather(way, step + 1, j).start()
        forward_blocks(NZ - 1 - step, 1 + step)
    gather(0, 3, 0).wait_recv()
    gather(1, 3, 1).wait_recv()
    forward_blocks(4, 4)

    for h in range(heads):
        total = lane_sum(tsum[h])
        a = (wsum[h] / total).astype(BF16)
        act[0, quad, :, h * HD : (h + 1) * HD] = a
        rtot[h] = 1.0 / total
        delta[h] = lane_sum(do[h].astype(F32) * a.astype(F32))
    shared(0, 1).start()
    shared(0, 0).start()

    def backward(b, h):
        p = ex[b, h] * twice(rtot[h])
        ds = (p * (dp[b, h] - twice(delta[h])) * scale).astype(BF16)
        dq[h] = dq[h] + dot(ds, kv[b, 0, h])
        ex[b, h, :, :HD] = dot(ds, q_low[h], FIRST)
        ex[b, h, :, HD:] = dot(p.astype(BF16), do[h], FIRST)

    def backward_blocks(first, count):
        def step(i, c):
            n = first + i // heads
            away = (n + 1) // 2
            b = lax.rem(me + 4 + lax.rem(n, 2) * (NZ - 2 * away) + away, NZ)
            backward(b, lax.rem(i, heads))
            return c

        lax.fori_loop(0, count * heads, step, 0)

    def scatter_step(step):
        for j in range(2):
            for way in range(2):
                if not goes(way, 3 - step, j):
                    continue
                b = lax.rem(me + (4 - step if way == 0 else 4 + step), NZ)
                added = step > 0 and goes(way, 4 - step, j)
                if added:
                    scatter(way, step - 1, j).wait_recv()
                for h in range(heads):
                    g = ex[b, h, :, j * HD : (j + 1) * HD]
                    if added:
                        g = g + rbuf[way, step - 1, j, h].astype(F32)
                    sbuf[way, step, j, h] = g.astype(BF16)
                scatter(way, step, j).start()

    def relay(group):
        shared(group, 1).wait_recv()
        shared(group, 2).start()

    def back(g, j, h):
        u = unit[j, h]
        return (g - lane_mean(g) - u * lane_mean(g * u)) * inv[j, h]

    backward_blocks(0, 1)
    scatter_step(0)
    backward_blocks(1, 7)
    for h in range(heads):
        a = back(dq[h], 0, h).astype(BF16)
        act[1, quad, :, h * HD : (h + 1) * HD] = a
        low[:, h * HD : (h + 1) * HD] = a
    shared(1, 1).start()
    shared(1, 0).start()
    scatter_step(1)
    relay(0)
    scatter_step(2)
    relay(1)
    scatter_step(3)

    for c in load_own:
        c.wait()
    for which in range(2):
        for k in range(3):
            transposed(k, which).wait_recv()
    for group in range(2):
        shared(group, 0).wait_recv()
        shared(group, 2).wait_recv()

    def weight_block(z, half):
        for i in range(2):
            group = 2 * half + i
            left = ct if group == 0 else ut
            acc = dot(left[0, z], act[group, 0])
            for m in range(1, NQ):
                acc = acc + dot(left[m, z], act[group, m])
            dwp[z, half, :, i * width : (i + 1) * width] = acc

    def weight_blocks(half):
        def step(i, c):
            weight_block(lax.rem(me + 5 + i, NZ), half)
            return c

        lax.fori_loop(0, NZ - 1, step, 0)

    def weight_step(step, half):
        for way in range(2):
            if not goes(way, 3 - step, half):
                continue
            z = lax.rem(me + (4 - step if way == 0 else 4 + step), NZ)
            g = dwp[z, half]
            if step > 0 and goes(way, 4 - step, half):
                weight_ring(way, step - 1, half).wait_recv()
                g = g + rdw[way, step - 1, half].astype(F32)
            sdw[way, step, half] = g.astype(BF16)
            weight_ring(way, step, half).start()

    weight_block(lax.rem(me + 4, NZ), 0)
    weight_step(0, 0)
    weight_blocks(0)

    for j in range(2):
        for way in range(2):
            scatter(way, 3, j).wait_recv()
        for h in range(heads):
            g = ex[me, h, :, j * HD : (j + 1) * HD]
            g = g + rbuf[0, 3, j, h].astype(F32) + rbuf[1, 3, j, h].astype(F32)
            if j == 0:
                g = back(g, 1, h)
            a = g.astype(BF16)
            act[2 + j, quad, :, h * HD : (h + 1) * HD] = a
            low[:, (j + 1) * width + h * HD : (j + 1) * width + (h + 1) * HD] = a
        shared(2 + j, 1).start()
        shared(2 + j, 0).start()
        weight_step(1 + j, 0)

    load_weight.wait()
    for c in load_normed:
        c.wait()
    own_unit[...] = nb[part]

    def inner(i, sums):
        x = lax.rem(xplace + 2 + i // 2, 4)
        t = 2 * x + lax.rem(i, 2)
        g = dot(low[...], w[pl.ds(pl.multiple_of(t * width, width), width), :], LAST)
        both = g * nb[t]
        nb[t] = g
        one, two = sums
        for k in range(heads):
            one = one + g[:, k * HD : (k + 1) * HD]
            two = two + both[:, k * HD : (k + 1) * HD]
        return one, two

    def inner_step(step):
        for half in range(2):
            for way in range(2):
                if step == 0 and half != way:
                    continue
                x = lax.rem(xplace + (2 - step if way == 0 else 2 + step), 4)
                g = nb[2 * x + half]
                if step > 0 and half == way:
                    xring(way, 0, half).wait_recv()
                    g = g + xr[way, 0, half].astype(F32)
                xs[way, step, half] = g.astype(BF16)
                xring(way, step, half).start()

    zero = jnp.zeros((low.shape[0], HD), F32)
    sums = lax.fori_loop(0, 2, inner, (zero, zero))
    inner_step(0)
    sums = lax.fori_loop(2, NT, inner, sums)
    relay(2)
    for i in range(2):
        stats[0, i * 8 : (i + 1) * 8, :] = jnp.transpose(lane_sum(sums[i]))[:8]
    for k in range(1, NT):
        stat(k).start()
    inner_step(1)
    relay(3)
    weight_step(3, 0)

    for group in range(2, 4):
        shared(group, 0).wait_recv()
        shared(group, 2).wait_recv()
    weight_block(lax.rem(me + 4, NZ), 1)
    weight_step(0, 1)
    weight_blocks(1)
    weight_step(1, 1)

    def arrived(half):
        g = nb[2 * xplace + half]
        return g + xr[0, 1, half].astype(F32) + xr[1, 1, half].astype(F32)

    for way in range(2):
        for half in range(2):
            xring(way, 1, half).wait_recv()
    ysend[...] = arrived(1 - yhalf).astype(BF16)
    ypair().start()
    weight_step(2, 1)
    for k in range(1, NT):
        stat(k).wait_recv()
    weight_step(3, 1)

    total = stats[0]
    for k in range(1, NT):
        total = total + stats[k]
    row_mean = []
    for i in range(2):
        row = jnp.broadcast_to(total[i * 8 : i * 8 + 1, :], (HD, total.shape[1]))
        row_mean.append(jnp.transpose(row) / features)
    ypair().wait_recv()
    share = arrived(yhalf) + yrecv[...].astype(F32)
    for k in range(heads):
        at = slice(k * HD, (k + 1) * HD)
        g = share[:, at] - row_mean[0] - own_unit[:, at] * row_mean[1]
        branch_out[:, at] = (g * inverse[...]).astype(BF16)

    for half in range(2):
        g = dwp[me, half]
        for way in range(2):
            weight_ring(way, 3, half).wait_recv()
            g = g + rdw[way, 3, half].astype(F32)
        dw_out[half] = g

    for step in range(4):
        for j in range(2):
            for way in range(2):
                if goes(way, step, j):
                    gather(way, step, j).wait_send()
                if goes(way, 3 - step, j):
                    scatter(way, step, j).wait_send()
                    weight_ring(way, step, j).wait_send()
    for which in range(2):
        for k in range(3):
            transposed(k, which).wait_send()
    for group in range(4):
        for k in range(3):
            shared(group, k).wait_send()
    for way in range(2):
        xring(way, 0, way).wait_send()
        for half in range(2):
            xring(way, 1, half).wait_send()
    ypair().wait_send()
    for k in range(1, NT):
        stat(k).wait_send()


def layer(proj, grad, inverse, normed, weight, unit_t, cot_t):
    rows, width = grad.shape
    heads = width // HD
    vmem = pl.BlockSpec(memory_space=pltpu.VMEM)
    hbm = pl.BlockSpec(memory_space=pl.ANY)
    one = (heads, rows, HD)
    own = unit_t.shape[2]
    dma = pltpu.SemaphoreType.DMA
    return pl.pallas_call(
        lambda *refs: layer_kernel(heads, *refs),
        out_shape=(
            jax.ShapeDtypeStruct((2, own, 2 * width), F32),
            jax.ShapeDtypeStruct((rows, width), BF16),
        ),
        in_specs=[vmem, vmem, vmem, hbm, hbm, hbm, hbm],
        out_specs=(vmem, vmem),
        scratch_shapes=[
            pltpu.VMEM(one, BF16),
            pltpu.VMEM(one, BF16),
            pltpu.VMEM((2, *one), F32),
            pltpu.VMEM((2, *one), F32),
            pltpu.VMEM((NZ, 2, *one), BF16),
            pltpu.VMEM((NZ, heads, rows, rows), F32),
            pltpu.VMEM((NZ, heads, rows, rows), F32),
            pltpu.VMEM(one, F32),
            pltpu.VMEM(one, F32),
            pltpu.VMEM(one, F32),
            pltpu.VMEM(one, F32),
            pltpu.VMEM(one, F32),
            pltpu.VMEM((2, 4, 2, *one), BF16),
            pltpu.VMEM((2, 4, 2, *one), BF16),
            pltpu.VMEM((4, NQ, rows, width), BF16),
            pltpu.VMEM((rows, 3 * width), BF16),
            pltpu.VMEM((NQ, NZ, own, rows), BF16),
            pltpu.VMEM((NQ, NZ, own, rows), BF16),
            pltpu.VMEM(weight.shape, BF16),
            pltpu.VMEM((NT, rows, width), F32),
            pltpu.VMEM((rows, width), F32),
            pltpu.VMEM((2, 4, 2, own, 2 * width), BF16),
            pltpu.VMEM((2, 4, 2, own, 2 * width), BF16),
            pltpu.VMEM((NZ, 2, own, 2 * width), F32),
            pltpu.VMEM((2, 2, 2, rows, width), BF16),
            pltpu.VMEM((2, 2, 2, rows, width), BF16),
            pltpu.VMEM((rows, width), BF16),
            pltpu.VMEM((rows, width), BF16),
            pltpu.VMEM((NT, 16, rows), F32),
            dma((2, 4, 2)),
            dma((2, 4, 2)),
            dma((2, 4, 2)),
            dma((2, 4, 2)),
            dma((3, 2)),
            dma((3, 2)),
            dma((4, 3)),
            dma((4, 3)),
            dma((2, 4, 2)),
            dma((2, 4, 2)),
            dma((2, 2, 2)),
            dma((2, 2, 2)),
            dma,
            dma,
            dma((NT - 1,)),
            dma((NT - 1,)),
            dma,
            dma((NT,)),
            dma((2,)),
        ],
        compiler_params=pltpu.CompilerParams(
            collective_id=0, has_side_effects=True, vmem_limit_bytes=62 * 1024 * 1024
        ),
    )(proj, grad, inverse, normed, weight, unit_t, cot_t)


def normalize(values):
    average = jnp.mean(values, axis=-1, keepdims=True)
    centered = values - average
    inverse = lax.rsqrt(jnp.mean(centered * centered, axis=-1, keepdims=True) + epsilon)
    return (centered * inverse, inverse)


def local(tokens, cotangent, qkv_weight, out_weight):
    rows = tokens.shape[1]
    width = out_weight.shape[1]
    own = qkv_weight.shape[0]
    grad_rows = cotangent[0]
    normed, inverse = normalize(tokens[0].astype(F32))
    unit_low = normed.astype(BF16)
    both = jnp.concatenate([qkv_weight.reshape(own, 3 * width), out_weight], axis=1)
    weights = lax.all_gather(both, ("seq", "dp"), axis=0, tiled=True)
    full_qkv, full_out = weights[:, : 3 * width], weights[:, 3 * width :]
    proj = dot(unit_low, full_qkv)
    grad = dot(grad_rows, full_out).astype(BF16)
    inverse = jnp.broadcast_to(inverse, (rows, HD))
    unit_t = unit_low.T.reshape(NZ, NQ, own, rows)
    cot_t = grad_rows.T.reshape(NZ, NQ, own, rows)
    dw, branch = layer(proj, grad, inverse, normed, full_qkv, unit_t, cot_t)
    out_grad = dw[0, :, :width]
    qkv_grad = jnp.stack([dw[0, :, width:], dw[1, :, :width], dw[1, :, width:]], axis=1)
    return (qkv_grad, out_grad, branch[None])


def solution(mesh):
    return jax.shard_map(
        local,
        mesh=mesh,
        in_specs=(
            P("dp", "seq", None),
            P("dp", "seq", None),
            P(("seq", "dp"), None, "tensor"),
            P(("seq", "dp"), "tensor"),
        ),
        out_specs=(
            P(("seq", "dp"), None, "tensor"),
            P(("seq", "dp"), "tensor"),
            P("dp", "seq", "tensor"),
        ),
        check_vma=False,
    )
```

time: 344 us -> 230 us (0.67)
  waiting for transfers between devices: 187 us -> 68.4 us
  Pallas kernels: 71.2 us -> 118 us
  other arithmetic: 20.5 us -> 5.65 us
  matrix products: 23.1 us -> 10.4 us
  blocking collectives: 11.5 us -> 0 us
  starting transfers between devices: 7.53 us -> 0.04 us
  local copies, waits for them, and re-layouts: 7 us -> 12.9 us
    reduce_scatter x1 -> x0, waiting for transfers between devices: 93.3 us -> none  [local(): lax.psum_scatter(jnp.concatenate([qkv_term, out_term[:, None, :]], axis=1...]
    pallas_call x1, Pallas kernels: 71.2 us -> 118 us  [layer(): pl.pallas_call(lambda *refs: layer_kernel(heads, *refs), out_shape=(jax.S...]
    all_to_all x1 -> x0, waiting for transfers between devices: 20.6 us -> none  [summed_on_arrival(): pieces = lax.all_to_all(split_up(shard, dim, size), axis, 0, 0, tiled=True)]
    dot_general x5 -> x2, matrix products: 23.1 us -> 10.4 us  [dot(): return lax.dot_general(a, b, dims, preferred_element_type=F32)]
    all_to_all x1 -> x0, blocking collectives: 11.5 us -> none  [copy_for_each(): return lax.all_to_all(copies, axis, split_axis=0, concat_axis=0, tiled=True)]
    concatenate x3 -> x1, other arithmetic: 10.1 us -> 1.62 us  [local(): jnp.concatenate([qkv_weight.reshape(own, 3 * width), out_weight], axis=1)]
    all_to_all x1 -> x0, starting transfers between devices: 7.45 us -> none  [summed_on_arrival(): pieces = lax.all_to_all(split_up(shard, dim, size), axis, 0, 0, tiled=True)]
    all_gather x1, waiting for transfers between devices: 73.3 us -> 68.3 us  [local(): weights = lax.all_gather(both, ('seq', 'dp'), axis=0, tiled=True)]
  transfers between devices with their start and end apart: 3 -> 1, of which waited for: 3 -> 1; matrix products, arithmetic and copies ran while one was open for 5% -> 3% of each run, Pallas kernels for 0% -> 0%
where the time goes in v2:
time: 230 us
  Pallas kernels  118 us (51%)
  waiting for transfers between devices  68.4 us (30%)
  between operations  14.1 us (6%)
  local copies, waits for them, and re-layouts  12.9 us (6%)
  matrix products  10.4 us (5%)
  other arithmetic  5.65 us (2%)
    pallas_call x1, Pallas kernels, layer(): pl.pallas_call(lambda *refs: layer_kernel(heads, *refs), out_shape=(jax.S...  118 us
    all_gather x1, waiting for transfers between devices, local(): weights = lax.all_gather(both, ('seq', 'dp'), axis=0, tiled=True)  68.3 us
    dot_general x2, matrix products, dot(): return lax.dot_general(a, b, dims, preferred_element_type=F32)  10.4 us
  transfers between devices with their start and end apart: 1, of which 1 were waited for; matrix products, arithmetic and copies ran while one was open for 3% of the time, Pallas kernels for 0%

profile of v2, /device:TPU:2, one launch (start us, length us, event | category | flops | bytes accessed | tf_op | source)
XLA Modules:
  0.0 229.8 jit_solution(9778678142720996910)
XLA Ops:
  7.2 0.0 copy-start
  7.2 0.0 all-gather.2.cloned.1.call-start
  7.2 1.1 copy.16
  8.3 1.6 pad_maximum_fusion.1
  9.9 0.0 all-gather.2.cloned.1.call-update
  9.9 2.6 %copy.14 = bf16[3072,256]{1,0:T(8,128)(2,1)} copy(bf16[3072,256]{0,1:T(8,128)(2,1)} %bitcast.45) | data formatting | bytes 3145728 | tf_op jit(solution)/shard_map/transpose | solution.py:594
  12.5 0.0 copy-done
  12.5 0.3 convert_reduce_fusion
  12.8 0.6 fusion.3
  13.4 2.4 %convert_bitcast_fusion.1 = (bf16[3072,256]{0,1:T(8,128)(2,1)S(1)}, f32[256,3072]{1,0:T(8,128)}) fusion(f32[256]{0:T(256)S(1)} %add_rsqrt_fusion, f32[256]{0:T(256)S(1)} %broadcast_multiply_fusion, bf16[1,256,3072]{2,1,0:T(8,128)(2,1)S(1)} %copy-done), kind=kLoop, calls=%fused_computation.11 | loop fusion | flops 3145728 | bytes 6293504 | tf_op jit(solution)/shard_map/transpose | solution.py:593
  15.8 1.6 copy.13
  17.4 68.3 %all-gather.2.cloned.1.call-done = bf16[3072,1536]{1,0:T(8,128)(2,1)} async-done(((bf16[96,1536]{1,0:T(8,128)(2,1)}), bf16[3072,1536]{1,0:T(8,128)(2,1)}) %all-gather.2.cloned.1.call-update) | async-done | bytes 9437200 | tf_op jit(solution)/shard_map/all_gather | solution.py:588
  85.7 0.0 slice-start
  85.7 3.9 %fusion.12.refs_1_ = bf16[256,384]{1,0:T(8,128)(2,1)} fusion(bf16[3072,1536]{1,0:T(8,128)(2,1)} %all-gather.2.cloned.1.call-done, bf16[1,256,3072]{2,1,0:T(8,128)(2,1)} %param.5), kind=kOutput, calls=%fused_computation.10 | convolution fusion | flops 604078080 | bytes 4128768 | tf_op jit(solution)/shard_map/dot_general | solution.py:21
  89.7 0.0 slice-start.1
  89.7 0.0 slice-start.2
  89.7 6.4 %fusion.17.refs_0_ = f32[256,1152]{1,0:T(8,128)} fusion(bf16[3072,1536]{1,0:T(8,128)(2,1)} %all-gather.2.cloned.1.call-done, bf16[1,256,3072]{2,1,0:T(8,128)(2,1)S(1)} %copy-done, f32[256]{0:T(256)S(1)} %add_rsqrt_fusion, f32[256]{0:T(256)S(1)} %broadcast_multiply_fusion), kind=kOutput, calls=%fused_computation.12 | convolution fusion | flops 1815085056 | bytes 9832448 | tf_op jit(solution)/shard_map/dot_general | solution.py:21
  96.1 0.0 slice-done
  96.1 0.0 slice-done.1
  96.1 0.0 slice-done.2
  96.1 3.5 %slice.24.refs_4_ = bf16[3072,1152]{1,0:T(8,128)(2,1)} slice(bf16[3072,1536]{1,0:T(8,128)(2,1)S(1)} %bitcast.44), slice={[0:3072], [0:1152]} | slice | bytes 14155776 | tf_op jit(solution)/shard_map/slice | solution.py:589
  99.6 0.8 broadcast_in_dim.4.refs_2_
  100.3 118.4 %shard_map.67 = (f32[2,96,768]{2,1,0:T(8,128)}, bf16[256,384]{1,0:T(8,128)(2,1)}) custom-call(f32[256,1152]{1,0:T(8,128)} %fusion.17.refs_0_, bf16[256,384]{1,0:T(8,128)(2,1)} %fusion.12.refs_1_, f32[256,128]{1,0:T(8,128)} %broadcast_in_dim.4.refs_2_, f32[256,3072]{1,0:T(8,128)} %get-tuple-element.8.refs_3_, bf16[3072,1152]{1,0:T(8,128)(2,1)} %slice.24.refs_4_, ...), custom_call_target="tpu_custom_call" | custom-call | tf_op jit(solution)/shard_map/pallas_call | solution.py:509
  218.7 1.8 slice_bitcast_fusion
  220.5 0.8 pad_maximum_fusion
  221.3 1.6 copy.18
  (3 shorter events, 0.0 us)
Async XLA Ops:
  7.2 5.4 %copy-start = (bf16[1,256,3072]{2,1,0:T(8,128)(2,1)S(1)}, bf16[1,256,3072]{2,1,0:T(8,128)(2,1)}, u32[]{:S(2)}) copy-start(bf16[1,256,3072]{2,1,0:T(8,128)(2,1)} %param.4) | copy-start | bytes 4718596
  7.2 78.5 %all-gather.2.cloned.1.call-start = ((), (), s32[]{:S(2)}) async-start(), calls=%async_computation | async-start | bytes 9732096 | tf_op jit(solution)/shard_map/all_gather | solution.py:588
  85.7 10.4 %slice-start = ((s8[9437184]{0:T(1024)(128)(4,1)}), s8[4194304]{0:T(1024)(128)(4,1)S(1)}, s32[]{:S(2)}) async-start(s8[9437184]{0:T(1024)(128)(4,1)} %bitcast.43), calls=%async_computation.1 | async-start | bytes 8388608
  89.7 6.4 %slice-start.1 = ((s8[9437184]{0:T(1024)(128)(4,1)}), s8[4194304]{0:T(1024)(128)(4,1)S(1)}, s32[]{:S(2)}) async-start(s8[9437184]{0:T(1024)(128)(4,1)} %bitcast.43), calls=%async_computation.2 | async-start | bytes 8388608
  89.7 6.4 %slice-start.2 = ((s8[9437184]{0:T(1024)(128)(4,1)}), s8[1048576]{0:T(1024)(128)(4,1)S(1)}, s32[]{:S(2)}) async-start(s8[9437184]{0:T(1024)(128)(4,1)} %bitcast.43), calls=%async_computation.3 | async-start | bytes 2097152
Sparse Core Ops, SparseCore 0:
  10.4 75.2 all-gather.1

commit v3 on v2

--- a/solution.py
+++ b/solution.py
@@ -37,8 +37,8 @@
     heads,
     proj,
     grad,
-    inverse,
-    normed,
+    norm,
+    tokens,
     weight,
     unit_t,
     cot_t,
@@ -63,8 +63,8 @@
     ut,
     ct,
     w,
+    tb,
     nb,
-    own_unit,
     sdw,
     rdw,
     dwp,
@@ -198,11 +198,13 @@
     def goes(way, step, j):
         return step < 3 or j == way
 
-    load_weight = pltpu.make_async_copy(weight, w, load_w)
-    load_weight.start()
-    load_normed = [
+    load_weight = [
+        pltpu.make_async_copy(weight.at[j // 2, :, j % 2], w.at[j], load_w.at[j])
+        for j in range(3)
+    ]
+    load_tokens = [
         pltpu.make_async_copy(
-            normed.at[:, t * width : (t + 1) * width], nb.at[t], load_n.at[t]
+            tokens.at[:, t * width : (t + 1) * width], tb.at[t], load_n.at[t]
         )
         for t in range(NT)
     ]
@@ -210,7 +212,7 @@
         pltpu.make_async_copy(unit_t.at[:, quad], ut.at[quad], load_t.at[0]),
         pltpu.make_async_copy(cot_t.at[:, quad], ct.at[quad], load_t.at[1]),
     ]
-    for c in load_normed + load_own:
+    for c in load_weight + load_tokens + load_own:
         c.start()
 
     for h in range(heads):
@@ -389,21 +391,23 @@
         shared(2 + j, 0).start()
         weight_step(1 + j, 0)
 
-    load_weight.wait()
-    for c in load_normed:
+    for c in load_weight + load_tokens:
         c.wait()
-    own_unit[...] = nb[part]
 
     def inner(i, sums):
         x = lax.rem(xplace + 2 + i // 2, 4)
         t = 2 * x + lax.rem(i, 2)
-        g = dot(low[...], w[pl.ds(pl.multiple_of(t * width, width), width), :], LAST)
-        both = g * nb[t]
+        blocks = pl.ds(pl.multiple_of(t * NQ, NQ), NQ)
+        g = dot(low[:, :width], w[0, blocks].reshape(width, width), LAST)
+        for j in range(1, 3):
+            left = low[:, j * width : (j + 1) * width]
+            g = g + dot(left, w[j, blocks].reshape(width, width), LAST)
         nb[t] = g
         one, two = sums
         for k in range(heads):
-            one = one + g[:, k * HD : (k + 1) * HD]
-            two = two + both[:, k * HD : (k + 1) * HD]
+            at = slice(k * HD, (k + 1) * HD)
+            one = one + g[:, at]
+            two = two + g[:, at] * ((tb[t, :, at].astype(F32) - norm[0]) * norm[1])
         return one, two
 
     def inner_step(step):
@@ -465,8 +469,9 @@
     share = arrived(yhalf) + yrecv[...].astype(F32)
     for k in range(heads):
         at = slice(k * HD, (k + 1) * HD)
-        g = share[:, at] - row_mean[0] - own_unit[:, at] * row_mean[1]
-        branch_out[:, at] = (g * inverse[...]).astype(BF16)
+        own_unit = (tb[part, :, at].astype(F32) - norm[0]) * norm[1]
+        g = share[:, at] - row_mean[0] - own_unit * row_mean[1]
+        branch_out[:, at] = (g * norm[1]).astype(BF16)
 
     for half in range(2):
         g = dwp[me, half]
@@ -498,7 +503,7 @@
         stat(k).wait_send()
 
 
-def layer(proj, grad, inverse, normed, weight, unit_t, cot_t):
+def layer(proj, grad, norm, tokens, weight, unit_t, cot_t):
     rows, width = grad.shape
     heads = width // HD
     vmem = pl.BlockSpec(memory_space=pltpu.VMEM)
@@ -533,9 +538,9 @@
             pltpu.VMEM((rows, 3 * width), BF16),
             pltpu.VMEM((NQ, NZ, own, rows), BF16),
             pltpu.VMEM((NQ, NZ, own, rows), BF16),
-            pltpu.VMEM(weight.shape, BF16),
+            pltpu.VMEM((3, NZ * NQ, own, width), BF16),
+            pltpu.VMEM((NT, rows, width), BF16),
             pltpu.VMEM((NT, rows, width), F32),
-            pltpu.VMEM((rows, width), F32),
             pltpu.VMEM((2, 4, 2, own, 2 * width), BF16),
             pltpu.VMEM((2, 4, 2, own, 2 * width), BF16),
             pltpu.VMEM((NZ, 2, own, 2 * width), F32),
@@ -560,39 +565,357 @@
             dma,
             dma((NT - 1,)),
             dma((NT - 1,)),
-            dma,
+            dma((3,)),
             dma((NT,)),
             dma((2,)),
         ],
         compiler_params=pltpu.CompilerParams(
             collective_id=0, has_side_effects=True, vmem_limit_bytes=62 * 1024 * 1024
         ),
-    )(proj, grad, inverse, normed, weight, unit_t, cot_t)
-
-
-def normalize(values):
-    average = jnp.mean(values, axis=-1, keepdims=True)
-    centered = values - average
-    inverse = lax.rsqrt(jnp.mean(centered * centered, axis=-1, keepdims=True) + epsilon)
-    return (centered * inverse, inverse)
+    )(proj, grad, norm, tokens, weight, unit_t, cot_t)
+
+
+def weights_kernel(
+    tokens,
+    cot,
+    own_qkv,
+    own_out,
+    proj_out,
+    grad_out,
+    norm_out,
+    ut_out,
+    ct_out,
+    g_out,
+    g,
+    tz,
+    uz,
+    cz,
+    acc,
+    send_za,
+    recv_za,
+    send_zb,
+    recv_zb,
+    send_ya,
+    recv_ya,
+    send_yb,
+    recv_yb,
+    send_da,
+    recv_da,
+    send_db,
+    recv_db,
+    load_g,
+    load_t,
+    load_c,
+    keep,
+):
+    me = lax.axis_index("seq")
+    quad = lax.axis_index("dp")
+    sides = (lax.rem(me + 1, NZ), lax.rem(me + NZ - 1, NZ))
+    mates = (quad + 1 - 2 * lax.rem(quad, 2), lax.rem(quad + 2, NQ), NQ - 1 - quad)
+    width = own_out.shape[1]
+    features = NZ * width
+
+    barrier = pltpu.get_barrier_semaphore()
+    for side in sides:
+        pl.semaphore_signal(barrier, inc=1, device_id={"seq": side}, device_id_type=MESH)
+    for mate in mates[:2]:
+        pl.semaphore_signal(barrier, inc=1, device_id={"dp": mate}, device_id_type=MESH)
+
+    mine = me * NQ + quad
+    load_own = [
+        pltpu.make_async_copy(own_qkv.at[0], g.at[0, mine, 0], load_g.at[0]),
+        pltpu.make_async_copy(own_qkv.at[1], g.at[0, mine, 1], load_g.at[1]),
+        pltpu.make_async_copy(own_qkv.at[2], g.at[1, mine, 0], load_g.at[2]),
+        pltpu.make_async_copy(own_out, g.at[1, mine, 1], load_g.at[3]),
+    ]
+    load_tok = [
+        pltpu.make_async_copy(tokens.at[:, z * width : (z + 1) * width], tz.at[z], load_t.at[z])
+        for z in range(NZ)
+    ]
+    load_cot = [
+        pltpu.make_async_copy(cot.at[:, z * width : (z + 1) * width], cz.at[z], load_c.at[z])
+        for z in range(NZ)
+    ]
+    for c in load_own + load_tok + load_cot:
+        c.start()
+
+    def remote(block, send, recv, where):
+        return pltpu.make_async_remote_copy(
+            src_ref=block,
+            dst_ref=block,
+            send_sem=send,
+            recv_sem=recv,
+            device_id=where,
+            device_id_type=MESH,
+        )
+
+    classes = (quad, mates[1])
+
+    def place(i):
+        if i == 0:
+            return me
+        if i >= 7:
+            return lax.rem(me + 4, NZ)
+        step, way = (i - 1) // 2, (i - 1) % 2
+        return lax.rem(me + (NZ - 1 - step if way == 0 else 1 + step), NZ)
+
+    def first_half(i, who):
+        b = place(i) * NQ + classes[who]
+        return g.at[0, b, i - 7] if i >= 7 else g.at[0, b]
+
+    def second_half(i, who):
+        return g.at[1, place(i) * NQ + classes[who]]
+
+    def index(way, step):
+        return 0 if step == 0 else 1 + 2 * (step - 1) + way
+
+    def za(way, step):
+        z = lax.rem(me + (NZ - step if way == 0 else step), NZ)
+        b = z * NQ + quad
+        return remote(
+            g.at[0, b, way] if step == 3 else g.at[0, b],
+            send_za.at[way, step],
+            recv_za.at[way, step],
+            {"seq": sides[way]},
+        )
+
+    def zb(who, way, step):
+        z = lax.rem(me + (NZ - step if way == 0 else step), NZ)
+        return remote(
+            g.at[1, z * NQ + classes[who]],
+            send_zb.at[who, way, step],
+            recv_zb.at[who, way, step],
+            {"seq": sides[way]},
+        )
+
+    def ya(i):
+        return remote(first_half(i, 0), send_ya.at[i], recv_ya.at[i], {"dp": mates[1]})
+
+    def yb():
+        return remote(second_half(0, 0), send_yb, recv_yb, {"dp": mates[1]})
+
+    def da(who, i):
+        return remote(
+            first_half(i, who), send_da.at[who, i], recv_da.at[who, i], {"dp": mates[0]}
+        )
+
+    def db(who, i):
+        return remote(
+            second_half(i, who), send_db.at[who, i], recv_db.at[who, i], {"dp": mates[0]}
+        )
+
+    for c in load_own:
+        c.wait()
+    pl.semaphore_wait(barrier, 4)
+    for way in range(2):
+        za(way, 0).start()
+    yb().start()
+    ya(0).start()
+    for way in range(2):
+        zb(0, way, 0).start()
+    da(0, 0).start()
+    db(0, 0).start()
+
+    rows = tz.shape[1]
+    zero = jnp.zeros((rows, HD), F32)
+    for c in load_tok:
+        c.wait()
+
+    def fold(a):
+        s = a[:, :HD]
+        for k in range(1, width // HD):
+            s = s + a[:, k * HD : (k + 1) * HD]
+        return s
+
+    def wide(a):
+        return jnp.concatenate([a] * (width // HD), axis=1)
+
+    def add_sum(z, s):
+        return s + fold(tz[z].astype(F32))
+
+    average = lane_sum(lax.fori_loop(0, NZ, add_sum, zero)) / features
+
+    def add_square(z, s):
+        c = tz[z].astype(F32) - wide(average)
+        return s + fold(c * c)
+
+    inverse = lax.rsqrt(lane_sum(lax.fori_loop(0, NZ, add_square, zero)) / features + epsilon)
+    norm_out[0] = average
+    norm_out[1] = inverse
+
+    yb().wait_recv()
+    for way in range(2):
+        zb(1, way, 0).start()
+    db(1, 0).start()
+
+    def low(z, c):
+        uz[z] = ((tz[z].astype(F32) - wide(average)) * wide(inverse)).astype(BF16)
+        return c
+
+    lax.fori_loop(0, NZ, low, 0)
+    for i in range(4):
+        acc[i] = jnp.zeros_like(acc[i])
+    for c in load_cot:
+        c.wait()
+
+    def turn(z, c):
+        for src, dst in ((uz, ut_out), (cz, ct_out)):
+            a = jnp.transpose(src[z])
+            dst[z] = a.reshape(dst.shape[1:])
+        return c
+
+    def product(z, slot):
+        blocks = pl.ds(pl.multiple_of(z * NQ, NQ), NQ)
+        for half in range(2):
+            for i in range(2):
+                w = g[half, blocks, i].reshape(width, width)
+                left = cz if half + i == 2 else uz
+                acc[2 * half + i] = acc[2 * half + i] + dot(left[z], w)
+            pltpu.make_async_copy(
+                g.at[half, blocks], g_out.at[half, blocks], keep.at[slot, half]
+            ).start()
+
+    def products(i):
+        if i == 0 or i >= 7:
+            product(place(i), 0 if i == 0 else 7)
+        else:
+            product(place(i), i)
+            product(place(i + 1), i + 1)
+
+    def other_core(i):
+        for who in range(2):
+            da(who, i).wait_recv()
+            if i < 8:
+                db(who, i).wait_recv()
+
+    def next_chip(i):
+        ya(i).wait_recv()
+        da(1, i).start()
+
+    for step in range(3):
+        for way in range(2):
+            i = index(way, step + 1)
+            za(way, step).wait_recv()
+            za(way, step + 1).start()
+            ya(i).start()
+            da(0, i).start()
+        for who in range(2):
+            for way in range(2):
+                zb(who, way, step).wait_recv()
+                if step < 2 or who == way:
+                    zb(who, way, step + 1).start()
+                db(who, index(way, step + 1)).start()
+        if step == 0:
+            next_chip(0)
+            other_core(0)
+            products(0)
+        else:
+            first = index(0, step)
+            for way in range(2):
+                next_chip(first + way)
+            for way in range(2):
+                other_core(first + way)
+            products(first)
+        lax.fori_loop(2 * step, 2 * step + 2, turn, 0)
+    for way in range(2):
+        za(way, 3).wait_recv()
+        ya(7 + way).start()
+        da(0, 7 + way).start()
+    lax.fori_loop(6, 8, turn, 0)
+    for i in range(5, 7):
+        next_chip(i)
+    for way in range(2):
+        zb(way, way, 3).wait_recv()
+        db(way, 7).start()
+    for i in range(5, 7):
+        other_core(i)
+    products(5)
+    for i in range(7, 9):
+        next_chip(i)
+    for i in range(7, 9):
+        other_core(i)
+    products(7)
+
+    for j in range(3):
+        proj_out[:, j * width : (j + 1) * width] = acc[j]
+    grad_out[...] = acc[3].astype(BF16)
+
+    for slot in range(NZ):
+        for half in range(2):
+            blocks = pl.ds(0, NQ)
+            pltpu.make_async_copy(
+                g.at[half, blocks], g_out.at[half, blocks], keep.at[slot, half]
+            ).wait()
+    for way in range(2):
+        for step in range(4):
+            za(way, step).wait_send()
+            for who in range(2):
+                if step < 3 or who == way:
+                    zb(who, way, step).wait_send()
+    for i in range(9):
+        ya(i).wait_send()
+        for who in range(2):
+            da(who, i).wait_send()
+            if i < 8:
+                db(who, i).wait_send()
+    yb().wait_send()
+
+
+def project(tokens, cot, own_qkv, own_out):
+    rows, features = tokens.shape
+    own, width = own_out.shape
+    vmem = pl.BlockSpec(memory_space=pltpu.VMEM)
+    hbm = pl.BlockSpec(memory_space=pl.ANY)
+    dma = pltpu.SemaphoreType.DMA
+    blocks = (2, NZ * NQ, 2, own, width)
+    turned = (NZ, NQ, own, rows)
+    return pl.pallas_call(
+        weights_kernel,
+        out_shape=(
+            jax.ShapeDtypeStruct((rows, 3 * width), F32),
+            jax.ShapeDtypeStruct((rows, width), BF16),
+            jax.ShapeDtypeStruct((2, rows, HD), F32),
+            jax.ShapeDtypeStruct(turned, BF16),
+            jax.ShapeDtypeStruct(turned, BF16),
+            jax.ShapeDtypeStruct(blocks, BF16),
+        ),
+        in_specs=[hbm] * 4,
+        out_specs=(vmem, vmem, vmem, vmem, vmem, hbm),
+        scratch_shapes=[
+            pltpu.VMEM(blocks, BF16),
+            pltpu.VMEM((NZ, rows, width), BF16),
+            pltpu.VMEM((NZ, rows, width), BF16),
+            pltpu.VMEM((NZ, rows, width), BF16),
+            pltpu.VMEM((4, rows, width), F32),
+            dma((2, 4)),
+            dma((2, 4)),
+            dma((2, 2, 4)),
+            dma((2, 2, 4)),
+            dma((9,)),
+            dma((9,)),
+            dma,
+            dma,
+            dma((2, 9)),
+            dma((2, 9)),
+            dma((2, 8)),
+            dma((2, 8)),
+            dma((4,)),
+            dma((NZ,)),
+            dma((NZ,)),
+            dma((NZ, 2)),
+        ],
+        compiler_params=pltpu.CompilerParams(
+            collective_id=1, has_side_effects=True, vmem_limit_bytes=60 * 1024 * 1024
+        ),
+    )(tokens, cot, own_qkv, own_out)
 
 
 def local(tokens, cotangent, qkv_weight, out_weight):
-    rows = tokens.shape[1]
     width = out_weight.shape[1]
-    own = qkv_weight.shape[0]
-    grad_rows = cotangent[0]
-    normed, inverse = normalize(tokens[0].astype(F32))
-    unit_low = normed.astype(BF16)
-    both = jnp.concatenate([qkv_weight.reshape(own, 3 * width), out_weight], axis=1)
-    weights = lax.all_gather(both, ("seq", "dp"), axis=0, tiled=True)
-    full_qkv, full_out = weights[:, : 3 * width], weights[:, 3 * width :]
-    proj = dot(unit_low, full_qkv)
-    grad = dot(grad_rows, full_out).astype(BF16)
-    inverse = jnp.broadcast_to(inverse, (rows, HD))
-    unit_t = unit_low.T.reshape(NZ, NQ, own, rows)
-    cot_t = grad_rows.T.reshape(NZ, NQ, own, rows)
-    dw, branch = layer(proj, grad, inverse, normed, full_qkv, unit_t, cot_t)
+    proj, grad, norm, unit_t, cot_t, weights = project(
+        tokens[0], cotangent[0], jnp.transpose(qkv_weight, (1, 0, 2)), out_weight
+    )
+    dw, branch = layer(proj, grad, norm, tokens[0], weights, unit_t, cot_t)
     out_grad = dw[0, :, :width]
     qkv_grad = jnp.stack([dw[0, :, width:], dw[1, :, :width], dw[1, :, width:]], axis=1)
     return (qkv_grad, out_grad, branch[None])

time: 230 us -> 170 us (0.74)
  waiting for transfers between devices: 68.4 us -> 0 us
  Pallas kernels: 118 us -> 166 us
  between operations: 14.1 us -> 0.66 us
  matrix products: 10.4 us -> 0 us
  local copies, waits for them, and re-layouts: 12.9 us -> 2.55 us
  other arithmetic: 5.65 us -> 0.79 us
    all_gather x1 -> x0, waiting for transfers between devices: 68.3 us -> none  [local(): weights = lax.all_gather(both, ('seq', 'dp'), axis=0, tiled=True)]
    pallas_call x0 -> x1, Pallas kernels: none -> 51.3 us  [project(): pl.pallas_call(weights_kernel, out_shape=(jax.ShapeDtypeStruct((rows, 3 *...]
    dot_general x2 -> x0, matrix products: 10.4 us -> none  [dot(): return lax.dot_general(a, b, dims, preferred_element_type=F32)]
    transpose x2 -> x0, local copies, waits for them, and re-layouts: 4.18 us -> none  [the longest x1 2.6 us: local(): cot_t = grad_rows.T.reshape(NZ, NQ, own, rows)]
    pallas_call x1, Pallas kernels: 118 us -> 115 us  [layer(): pl.pallas_call(lambda *refs: layer_kernel(heads, *refs), out_shape=(jax.S...]
    slice x1 -> x0, local copies, waits for them, and re-layouts: 3.45 us -> none  [local(): full_qkv, full_out = (weights[:, :3 * width], weights[:, 3 * width:])]
    transpose x1 -> x0, other arithmetic: 2.37 us -> none  [local(): unit_t = unit_low.T.reshape(NZ, NQ, own, rows)]
  transfers between devices with their start and end apart: 1 -> 0, of which waited for: 1 -> 0; matrix products, arithmetic and copies ran while one was open for 3% -> 0% of each run, Pallas kernels for 0% -> 0%
where the time goes in v3:
time: 170 us
  Pallas kernels  166 us (98%)
  local copies, waits for them, and re-layouts  2.55 us (1%)
    pallas_call x1, Pallas kernels, layer(): pl.pallas_call(lambda *refs: layer_kernel(heads, *refs), out_shape=(jax.S...  115 us
    pallas_call x1, Pallas kernels, project(): pl.pallas_call(weights_kernel, out_shape=(jax.ShapeDtypeStruct((rows, 3 *...  51.3 us

profile of v3, /device:TPU:2, one launch (start us, length us, event | category | flops | bytes accessed | tf_op | source)
XLA Modules:
  0.0 169.9 jit_solution(15800922951585278302)
XLA Ops:
  0.6 51.3 %shard_map.67 = (f32[256,1152]{1,0:T(8,128)}, bf16[256,384]{1,0:T(8,128)(2,1)}, f32[2,256,128]{2,1,0:T(8,128)}, bf16[8,4,96,256]{3,2,1,0:T(8,128)(2,1)}, bf16[8,...) custom-call(bf16[256,3072]{1,0:T(8,128)(2,1)} %bitcast.12, bf16[256,3072]{1,0:T(8,128)(2,1)} %bitcast.14, ...), custom_call_target="tpu_custom_call" | custom-call | tf_op jit(solution)/shard_map/pallas_call | solution.py:872
  51.9 114.6 %shard_map.68 = (f32[2,96,768]{2,1,0:T(8,128)}, bf16[256,384]{1,0:T(8,128)(2,1)}) custom-call(f32[256,1152]{1,0:T(8,128)} %get-tuple-element.11.refs_0_, bf16[256,384]{1,0:T(8,128)(2,1)} %get-tuple-element.12.refs_1_, f32[2,256,128]{2,1,0:T(8,128)} %get-tuple-element.13.refs_2_, bf16[256,3072]{1,0:T(8,128)(2,1)} %bitcast.13, ...), custom_call_target="tpu_custom_call" | custom-call | tf_op jit(solution)/shard_map/pallas_call | solution.py:514
  166.5 0.0 copy-start
  166.5 1.9 %slice_bitcast_fusion = (f32[96,384]{1,0:T(8,128)}, f32[96,1,384]{2,0,1:T(8,128)S(1)}, f32[96,1,384]{2,0,1:T(8,128)S(1)}, f32[96,1,384]{2,0,1:T(8,128)S(1)}) fusion(f32[2,96,768]{2,1,0:T(8,128)} %get-tuple-element.17), kind=kLoop, calls=%fused_computation.1 | loop fusion | bytes 1179648 | tf_op jit(solution)/shard_map/squeeze | solution.py:919
  168.4 0.8 pad_maximum_fusion
  169.2 0.0 copy-done
  169.2 0.7 copy.8
Async XLA Ops:
  166.5 2.7 %copy-start = (bf16[256,384]{1,0:T(8,128)(2,1)S(1)}, bf16[256,384]{1,0:T(8,128)(2,1)}, u32[]{:S(2)}) copy-start(bf16[256,384]{1,0:T(8,128)(2,1)} %get-tuple-element.18) | copy-start | bytes 589828

commit v4 on v2

v4 whole, which is shorter than its diff:
```python
import jax
import jax.numpy as jnp
from jax import lax
from jax.experimental import pallas as pl
from jax.experimental.pallas import tpu as pltpu
from jax.sharding import PartitionSpec as P

HD = 128
NZ = 8
NT = 8
NQ = 4
MESH = pl.DeviceIdType.MESH
F32 = jnp.float32
BF16 = jnp.bfloat16
LAST = (((1,), (1,)), ((), ()))
FIRST = (((0,), (0,)), ((), ()))
epsilon = 1e-06


def dot(a, b, dims=(((1,), (0,)), ((), ()))):
    return lax.dot_general(a, b, dims, preferred_element_type=F32)


def twice(a):
    return jnp.concatenate([a, a], axis=1)


def lane_mean(a):
    return jnp.broadcast_to(jnp.mean(a, axis=1, keepdims=True), a.shape)


def lane_sum(a):
    return jnp.broadcast_to(jnp.sum(a, axis=1, keepdims=True), a.shape)


def layer_kernel(
    heads,
    tokens,
    cot,
    own_qkv,
    own_out,
    qkv_out,
    out_out,
    branch_out,
    q_low,
    do,
    unit,
    inv,
    kv,
    ex,
    dp,
    wsum,
    tsum,
    rtot,
    delta,
    dq,
    sbuf,
    rbuf,
    act,
    low,
    ut,
    ct,
    us,
    cs,
    g,
    tb,
    nb,
    norm,
    sdw,
    rdw,
    dwp,
    xs,
    xr,
    ysend,
    yrecv,
    stats,
    send_ag,
    recv_ag,
    send_rs,
    recv_rs,
    send_tr,
    recv_tr,
    send_act,
    recv_act,
    send_dw,
    recv_dw,
    send_x,
    recv_x,
    send_y,
    recv_y,
    send_st,
    recv_st,
    send_za,
    recv_za,
    send_zb,
    recv_zb,
    send_ya,
    recv_ya,
    send_yb,
    recv_yb,
    send_da,
    recv_da,
    send_db,
    recv_db,
    load_g,
    load_t,
    load_c,
):
    me = lax.axis_index("seq")
    quad = lax.axis_index("dp")
    part = lax.axis_index("tensor")
    sides = (lax.rem(me + 1, NZ), lax.rem(me + NZ - 1, NZ))
    mates = (quad + 1 - 2 * lax.rem(quad, 2), lax.rem(quad + 2, NQ), NQ - 1 - quad)
    xsides = (lax.rem(part + 2, NT), lax.rem(part + NT - 2, NT))
    ymate = part + 1 - 2 * lax.rem(part, 2)
    yhalf = lax.rem(part, 2)
    xplace = part // 2
    scale = HD ** (-0.5)
    width = heads * HD
    features = NT * width

    barrier = pltpu.get_barrier_semaphore()
    for side in sides:
        pl.semaphore_signal(barrier, inc=1, device_id={"seq": side}, device_id_type=MESH)
    for mate in mates:
        pl.semaphore_signal(barrier, inc=1, device_id={"dp": mate}, device_id_type=MESH)
    for k in range(1, NT):
        pl.semaphore_signal(
            barrier, inc=1, device_id={"tensor": lax.rem(part + k, NT)}, device_id_type=MESH
        )

    def remote(src, dst, send, recv, where):
        return pltpu.make_async_remote_copy(
            src_ref=src,
            dst_ref=dst,
            send_sem=send,
            recv_sem=recv,
            device_id=where,
            device_id_type=MESH,
        )

    def gather(way, step, j):
        b = lax.rem(me + (NZ - step if way == 0 else step), NZ)
        return remote(
            kv.at[b, j],
            kv.at[b, j],
            send_ag.at[way, step, j],
            recv_ag.at[way, step, j],
            {"seq": sides[way]},
        )

    def scatter(way, step, j):
        return remote(
            sbuf.at[way, step, j],
            rbuf.at[way, step, j],
            send_rs.at[way, step, j],
            recv_rs.at[way, step, j],
            {"seq": sides[way]},
        )

    def weight_ring(way, step, group):
        return remote(
            sdw.at[way, step, group],
            rdw.at[way, step, group],
            send_dw.at[way, step, group],
            recv_dw.at[way, step, group],
            {"seq": sides[way]},
        )

    def transposed(k, which):
        src, dst = ((us, ut), (cs, ct))[which]
        return remote(
            src.at[:, mates[k]],
            dst.at[quad],
            send_tr.at[k, which],
            recv_tr.at[k, which],
            {"dp": mates[k]},
        )

    def shared(group, k):
        block = act.at[group, quad if k < 2 else mates[1]]
        return remote(
            block,
            block,
            send_act.at[group, k],
            recv_act.at[group, k],
            {"dp": mates[1] if k == 1 else mates[0]},
        )

    def xring(way, step, half):
        return remote(
            xs.at[way, step, half],
            xr.at[way, step, half],
            send_x.at[way, step, half],
            recv_x.at[way, step, half],
            {"tensor": xsides[way]},
        )

    def ypair():
        return remote(ysend, yrecv, send_y, recv_y, {"tensor": ymate})

    def stat(k):
        return remote(
            stats.at[0],
            stats.at[k],
            send_st.at[k - 1],
            recv_st.at[k - 1],
            {"tensor": lax.rem(part + k, NT)},
        )

    def goes(way, step, j):
        return step < 3 or j % 2 == way

    mine = me * NQ + quad
    load_own = [
        pltpu.make_async_copy(own_qkv.at[1], g.at[0, 0, mine], load_g.at[0]),
        pltpu.make_async_copy(own_qkv.at[2], g.at[0, 1, mine], load_g.at[1]),
        pltpu.make_async_copy(own_qkv.at[0], g.at[1, 0, mine], load_g.at[2]),
        pltpu.make_async_copy(own_out, g.at[1, 1, mine], load_g.at[3]),
    ]
    load_tokens = [
        pltpu.make_async_copy(tokens.at[:, z * width : (z + 1) * width], tb.at[z], load_t.at[z])
        for z in range(NZ)
    ]
    load_cot = [
        pltpu.make_async_copy(
            cot.at[:, (z * heads + h) * HD : (z * heads + h + 1) * HD],
            sbuf.at[z // 4, z % 4, 1, h],
            load_c.at[z, h],
        )
        for z in range(NZ)
        for h in range(heads)
    ]
    for c in load_own + load_tokens + load_cot:
        c.start()

    classes = (quad, mates[1])
    half_rows = own_out.shape[0] // 2

    def place(i):
        if i == 0:
            return me
        if i >= 7:
            return lax.rem(me + 4, NZ)
        step, way = (i - 1) // 2, (i - 1) % 2
        return lax.rem(me + (NZ - 1 - step if way == 0 else 1 + step), NZ)

    def first_array(p, i, who):
        b = place(i) * NQ + classes[who]
        if i >= 7:
            return g.at[p, 0, b, (i - 7) * half_rows : (i - 6) * half_rows]
        return g.at[p, 0, b]

    def second_array(p, i, who):
        return g.at[p, 1, place(i) * NQ + classes[who]]

    def index(way, step):
        return 0 if step == 0 else 1 + 2 * (step - 1) + way

    def same(block, send, recv, where):
        return remote(block, block, send, recv, where)

    def za(p, way, step):
        return same(
            g.at[p, 0, lax.rem(me + (NZ - step if way == 0 else step), NZ) * NQ + quad]
            if step < 3
            else g.at[
                p,
                0,
                lax.rem(me + (NZ - step if way == 0 else step), NZ) * NQ + quad,
                way * half_rows : (way + 1) * half_rows,
            ],
            send_za.at[p, way, step],
            recv_za.at[p, way, step],
            {"seq": sides[way]},
        )

    def zb(p, who, way, step):
        z = lax.rem(me + (NZ - step if way == 0 else step), NZ)
        return same(
            g.at[p, 1, z * NQ + classes[who]],
            send_zb.at[p, who, way, step],
            recv_zb.at[p, who, way, step],
            {"seq": sides[way]},
        )

    def ya(p, i):
        return same(
            first_array(p, i, 0), send_ya.at[p, i], recv_ya.at[p, i], {"dp": mates[1]}
        )

    def yb(p):
        return same(second_array(p, 0, 0), send_yb.at[p], recv_yb.at[p], {"dp": mates[1]})

    def da(p, who, i):
        return same(
            first_array(p, i, who),
            send_da.at[p, who, i],
            recv_da.at[p, who, i],
            {"dp": mates[0]},
        )

    def db(p, who, i):
        return same(
            second_array(p, i, who),
            send_db.at[p, who, i],
            recv_db.at[p, who, i],
            {"dp": mates[0]},
        )

    for c in load_own:
        c.wait()
    pl.semaphore_wait(barrier, 2 + 3 + NT - 1)
    for p in range(2):
        for way in range(2):
            za(p, way, 0).start()
        yb(p).start()
        ya(p, 0).start()
        for way in range(2):
            zb(p, 0, way, 0).start()
        da(p, 0, 0).start()
        db(p, 0, 0).start()

    rows = tb.shape[1]
    blank = jnp.zeros((rows, HD), F32)
    for c in load_tokens:
        c.wait()

    def fold(a):
        s = a[:, :HD]
        for k in range(1, heads):
            s = s + a[:, k * HD : (k + 1) * HD]
        return s

    def wide(a):
        return jnp.concatenate([a] * heads, axis=1)

    def add_sum(z, s):
        return s + fold(tb[z].astype(F32))

    average = lane_sum(lax.fori_loop(0, NZ, add_sum, blank)) / features

    def add_square(z, s):
        c = tb[z].astype(F32) - wide(average)
        return s + fold(c * c)

    norm[0] = average
    norm[1] = lax.rsqrt(lane_sum(lax.fori_loop(0, NZ, add_square, blank)) / features + epsilon)

    for p in range(2):
        yb(p).wait_recv()
        for way in range(2):
            zb(p, 1, way, 0).start()
        db(p, 1, 0).start()

    def lower(z, c):
        for h in range(heads):
            a = tb[z, :, h * HD : (h + 1) * HD].astype(F32)
            sbuf[z // 4, lax.rem(z, 4), 0, h] = ((a - norm[0]) * norm[1]).astype(BF16)
        return c

    lax.fori_loop(0, NZ, lower, 0)
    for i in range(4):
        nb[i] = jnp.zeros_like(nb[i])
    for c in load_cot:
        c.wait()

    def low_rows(z, which):
        return jnp.concatenate(
            [sbuf[z // 4, lax.rem(z, 4), which, h] for h in range(heads)], axis=1
        )

    def turn(first, count):
        def step(z, c):
            for which, (dst, kept) in enumerate(((us, ut), (cs, ct))):
                dst[z] = jnp.transpose(low_rows(z, which)).reshape(dst.shape[1:])
                kept[quad, z] = dst[z, quad]
            return c

        lax.fori_loop(first, first + count, step, 0)

    def products(p, i):
        def one(z):
            blocks = pl.ds(pl.multiple_of(z * NQ, NQ), NQ)
            for j in range(2):
                left = low_rows(z, 1 if p + j == 2 else 0)
                nb[2 * p + j] = nb[2 * p + j] + dot(left, g[p, j, blocks].reshape(width, width))

        if i == 0 or i >= 7:
            one(place(i))
        else:

            def step(n, c):
                d = (i + 1) // 2
                one(lax.rem(me + NZ - d + 2 * d * n, NZ))
                return c

            lax.fori_loop(0, 2, step, 0)

    def other_core(p, i):
        for who in range(2):
            da(p, who, i).wait_recv()
            if i < 8:
                db(p, who, i).wait_recv()

    def next_chip(p, i):
        ya(p, i).wait_recv()
        da(p, 1, i).start()

    def ring_step(p, step):
        for way in range(2):
            i = index(way, step + 1)
            za(p, way, step).wait_recv()
            za(p, way, step + 1).start()
            ya(p, i).start()
            da(p, 0, i).start()
        for who in range(2):
            for way in range(2):
                zb(p, who, way, step).wait_recv()
                if step < 2 or who == way:
                    zb(p, who, way, step + 1).start()
                db(p, who, index(way, step + 1)).start()

    def ring_last(p):
        for way in range(2):
            za(p, way, 3).wait_recv()
            ya(p, 7 + way).start()
            da(p, 0, 7 + way).start()
        for way in range(2):
            zb(p, way, way, 3).wait_recv()
            db(p, way, 7).start()

    def settle(p, step):
        these = (0,) if step == 0 else (2 * step - 1, 2 * step) if step < 4 else (7, 8)
        for i in these:
            next_chip(p, i)
        for i in these:
            other_core(p, i)
        products(p, these[0])

    def normal(a, j, h):
        c = a - lane_mean(a)
        r = lax.rsqrt(lane_mean(c * c) + epsilon)
        u = c * r
        unit[j, h] = u
        inv[j, h] = r
        return u.astype(BF16)

    ring_step(0, 0)
    turn(0, 2)
    settle(0, 0)
    ring_step(0, 1)
    settle(0, 1)
    turn(2, 2)
    ring_step(1, 0)
    ring_step(0, 2)
    settle(0, 2)
    turn(4, 2)
    ring_step(1, 1)
    settle(1, 0)
    ring_last(0)
    settle(0, 3)
    ring_step(1, 2)
    settle(0, 4)
    for h in range(heads):
        at = slice(h * HD, (h + 1) * HD)
        kv[me, 0, h] = normal(nb[0, :, at], 1, h)
        kv[me, 1, h] = nb[1, :, at].astype(BF16)
    for j in range(2):
        for way in range(2):
            gather(way, 0, j).start()
    settle(1, 1)
    settle(1, 2)
    turn(6, 2)
    ring_last(1)
    for which in range(2):
        for k in range(3):
            transposed(k, which).start()
    settle(1, 3)
    settle(1, 4)
    for h in range(heads):
        at = slice(h * HD, (h + 1) * HD)
        q_low[h] = normal(nb[2, :, at], 0, h)
        do[h] = nb[3, :, at].astype(BF16)
        wsum[h] = jnp.zeros_like(wsum[h])
        tsum[h] = jnp.zeros_like(tsum[h])
        dq[h] = jnp.zeros_like(dq[h])

    def forward(b, h):
        k = kv[b, 0, h]
        v = kv[b, 1, h]
        e = jnp.exp(dot(q_low[h], k, LAST) * scale)
        ex[b, h] = e
        tsum[h] = tsum[h] + (e[:, :HD] + e[:, HD:])
        wsum[h] = wsum[h] + dot(e.astype(BF16), v)
        dp[b, h] = dot(do[h], v, LAST)

    def forward_blocks(ahead, behind):
        def step(i, c):
            b = lax.rem(me + ahead + (i // heads) * (behind - ahead), NZ)
            forward(b, lax.rem(i, heads))
            return c

        lax.fori_loop(0, heads if ahead == behind else 2 * heads, step, 0)

    forward_blocks(0, 0)
    for step in range(3):
        for j in range(2):
            for way in range(2):
                gather(way, step, j).wait_recv()
                if goes(way, step + 1, j):
                    gather(way, step + 1, j).start()
        forward_blocks(NZ - 1 - step, 1 + step)
    gather(0, 3, 0).wait_recv()
    gather(1, 3, 1).wait_recv()
    forward_blocks(4, 4)

    for h in range(heads):
        total = lane_sum(tsum[h])
        a = (wsum[h] / total).astype(BF16)
        act[0, quad, :, h * HD : (h + 1) * HD] = a
        rtot[h] = 1.0 / total
        delta[h] = lane_sum(do[h].astype(F32) * a.astype(F32))
    shared(0, 1).start()
    shared(0, 0).start()

    def backward(b, h):
        p = ex[b, h] * twice(rtot[h])
        ds = (p * (dp[b, h] - twice(delta[h])) * scale).astype(BF16)
        dq[h] = dq[h] + dot(ds, kv[b, 0, h])
        ex[b, h, :, :HD] = dot(ds, q_low[h], FIRST)
        ex[b, h, :, HD:] = dot(p.astype(BF16), do[h], FIRST)

    def backward_blocks(first, count):
        def step(i, c):
            n = first + i // heads
            away = (n + 1) // 2
            b = lax.rem(me + 4 + lax.rem(n, 2) * (NZ - 2 * away) + away, NZ)
            backward(b, lax.rem(i, heads))
            return c

        lax.fori_loop(0, count * heads, step, 0)

    def scatter_step(step):
        for j in range(2):
            for way in range(2):
                if not goes(way, 3 - step, j):
                    continue
                b = lax.rem(me + (4 - step if way == 0 else 4 + step), NZ)
                added = step > 0 and goes(way, 4 - step, j)
                if added:
                    scatter(way, step - 1, j).wait_recv()
                for h in range(heads):
                    val = ex[b, h, :, j * HD : (j + 1) * HD]
                    if added:
                        val = val + rbuf[way, step - 1, j, h].astype(F32)
                    sbuf[way, step, j, h] = val.astype(BF16)
                scatter(way, step, j).start()

    def relay(group):
        shared(group, 1).wait_recv()
        shared(group, 2).start()

    def back(val, j, h):
        u = unit[j, h]
        return (val - lane_mean(val) - u * lane_mean(val * u)) * inv[j, h]

    backward_blocks(0, 1)
    scatter_step(0)
    backward_blocks(1, 7)
    for h in range(heads):
        a = back(dq[h], 0, h).astype(BF16)
        act[1, quad, :, h * HD : (h + 1) * HD] = a
        low[:, h * HD : (h + 1) * HD] = a
    shared(1, 1).start()
    shared(1, 0).start()
    scatter_step(1)
    relay(0)
    scatter_step(2)
    relay(1)
    scatter_step(3)

    for which in range(2):
        for k in range(3):
            transposed(k, which).wait_recv()
    for group in range(2):
        shared(group, 0).wait_recv()
        shared(group, 2).wait_recv()

    def weight_block(z, group):
        left = ct if group == 0 else ut
        acc = dot(left[0, z], act[group, 0])
        for m in range(1, NQ):
            acc = acc + dot(left[m, z], act[group, m])
        dwp[z, group] = acc

    def weight_blocks(*groups):
        def step(i, c):
            for group in groups:
                weight_block(lax.rem(me + 5 + i, NZ), group)
            return c

        lax.fori_loop(0, NZ - 1, step, 0)

    def weight_step(step, group):
        for way in range(2):
            if not goes(way, 3 - step, group):
                continue
            z = lax.rem(me + (4 - step if way == 0 else 4 + step), NZ)
            val = dwp[z, group]
            if step > 0 and goes(way, 4 - step, group):
                weight_ring(way, step - 1, group).wait_recv()
                val = val + rdw[way, step - 1, group].astype(F32)
            sdw[way, step, group] = val.astype(BF16)
            weight_ring(way, step, group).start()

    for group in range(2):
        weight_block(lax.rem(me + 4, NZ), group)
        weight_step(0, group)
    weight_blocks(0, 1)

    for j in range(2):
        for way in range(2):
            scatter(way, 3, j).wait_recv()
        for h in range(heads):
            val = ex[me, h, :, j * HD : (j + 1) * HD]
            val = val + rbuf[0, 3, j, h].astype(F32) + rbuf[1, 3, j, h].astype(F32)
            if j == 0:
                val = back(val, 1, h)
            a = val.astype(BF16)
            act[2 + j, quad, :, h * HD : (h + 1) * HD] = a
            low[:, (j + 1) * width + h * HD : (j + 1) * width + (h + 1) * HD] = a
        shared(2 + j, 1).start()
        shared(2 + j, 0).start()
        for group in range(2):
            weight_step(1 + j, group)

    def inner(n, sums):
        x = lax.rem(xplace + 2 + n // 2, 4)
        t = 2 * x + lax.rem(n, 2)
        blocks = pl.ds(pl.multiple_of(t * NQ, NQ), NQ)
        a = jnp.zeros_like(nb[t])
        for j, (p, i) in enumerate(((1, 0), (0, 0), (0, 1))):
            left = low[:, j * width : (j + 1) * width]
            a = a + dot(left, g[p, i, blocks].reshape(width, width), LAST)
        nb[t] = a
        one, two = sums
        for k in range(heads):
            at = slice(k * HD, (k + 1) * HD)
            one = one + a[:, at]
            two = two + a[:, at] * ((tb[t, :, at].astype(F32) - norm[0]) * norm[1])
        return one, two

    def piece(x, half):
        return nb[2 * x + (1 - yhalf if half == 0 else yhalf)]

    def inner_step(step):
        for half in range(2):
            for way in range(2):
                if step == 0 and half != way:
                    continue
                x = lax.rem(xplace + (2 - step if way == 0 else 2 + step), 4)
                val = piece(x, half)
                if step > 0 and half == way:
                    xring(way, 0, half).wait_recv()
                    val = val + xr[way, 0, half].astype(F32)
                xs[way, step, half] = val.astype(BF16)
                xring(way, step, half).start()

    def arrived(half):
        for way in range(2):
            xring(way, 1, half).wait_recv()
        val = piece(xplace, half)
        return val + xr[0, 1, half].astype(F32) + xr[1, 1, half].astype(F32)

    far = lax.rem(me + 4, NZ)
    zero = jnp.zeros((low.shape[0], HD), F32)
    sums = lax.fori_loop(0, 2, inner, (zero, zero))
    inner_step(0)
    sums = lax.fori_loop(2, 4, inner, sums)
    relay(2)
    sums = lax.fori_loop(4, NT, inner, sums)
    shared(2, 0).wait_recv()
    shared(2, 2).wait_recv()
    weight_block(far, 2)
    weight_step(0, 2)
    for i in range(2):
        stats[0, i * 8 : (i + 1) * 8, :] = jnp.transpose(lane_sum(sums[i]))[:8]
    for k in range(1, NT):
        stat(k).start()
    relay(3)
    weight_blocks(2)
    for group in range(2):
        weight_step(3, group)
    inner_step(1)
    weight_step(1, 2)
    shared(3, 0).wait_recv()
    shared(3, 2).wait_recv()
    weight_block(far, 3)
    weight_step(0, 3)
    weight_blocks(3)
    weight_step(2, 2)
    ysend[...] = arrived(0).astype(BF16)
    ypair().start()
    weight_step(1, 3)
    weight_step(3, 2)
    weight_step(2, 3)
    for k in range(1, NT):
        stat(k).wait_recv()
    total = stats[0]
    for k in range(1, NT):
        total = total + stats[k]
    row_mean = []
    for i in range(2):
        row = jnp.broadcast_to(total[i * 8 : i * 8 + 1, :], (HD, total.shape[1]))
        row_mean.append(jnp.transpose(row) / features)
    share = arrived(1)
    weight_step(3, 3)

    ypair().wait_recv()
    share = share + yrecv[...].astype(F32)
    for k in range(heads):
        at = slice(k * HD, (k + 1) * HD)
        own_unit = (tb[part, :, at].astype(F32) - norm[0]) * norm[1]
        val = share[:, at] - row_mean[0] - own_unit * row_mean[1]
        branch_out[:, at] = (val * norm[1]).astype(BF16)

    for group in range(4):
        val = dwp[me, group]
        for way in range(2):
            weight_ring(way, 3, group).wait_recv()
            val = val + rdw[way, 3, group].astype(F32)
        if group == 0:
            out_out[...] = val
        else:
            qkv_out[group - 1] = val

    for p in range(2):
        for way in range(2):
            for step in range(4):
                za(p, way, step).wait_send()
                for who in range(2):
                    if step < 3 or who == way:
                        zb(p, who, way, step).wait_send()
        for i in range(9):
            ya(p, i).wait_send()
            for who in range(2):
                da(p, who, i).wait_send()
                if i < 8:
                    db(p, who, i).wait_send()
        yb(p).wait_send()
    for step in range(4):
        for j in range(2):
            for way in range(2):
                if goes(way, step, j):
                    gather(way, step, j).wait_send()
                if goes(way, 3 - step, j):
                    scatter(way, step, j).wait_send()
                    weight_ring(way, step, j).wait_send()
                    weight_ring(way, step, j + 2).wait_send()
    for which in range(2):
        for k in range(3):
            transposed(k, which).wait_send()
    for group in range(4):
        for k in range(3):
            shared(group, k).wait_send()
    for way in range(2):
        xring(way, 0, way).wait_send()
        for half in range(2):
            xring(way, 1, half).wait_send()
    ypair().wait_send()
    for k in range(1, NT):
        stat(k).wait_send()


def layer(tokens, cot, own_qkv, own_out):
    rows = tokens.shape[0]
    own, width = own_out.shape
    heads = width // HD
    vmem = pl.BlockSpec(memory_space=pltpu.VMEM)
    hbm = pl.BlockSpec(memory_space=pl.ANY)
    one = (heads, rows, HD)
    dma = pltpu.SemaphoreType.DMA
    return pl.pallas_call(
        lambda *refs: layer_kernel(heads, *refs),
        out_shape=(
            jax.ShapeDtypeStruct((3, own, width), F32),
            jax.ShapeDtypeStruct((own, width), F32),
            jax.ShapeDtypeStruct((rows, width), BF16),
        ),
        in_specs=[hbm] * 4,
        out_specs=(vmem, vmem, vmem),
        scratch_shapes=[
            pltpu.VMEM(one, BF16),
            pltpu.VMEM(one, BF16),
            pltpu.VMEM((2, *one), F32),
            pltpu.VMEM((2, *one), F32),
            pltpu.VMEM((NZ, 2, *one), BF16),
            pltpu.VMEM((NZ, heads, rows, rows), F32),
            pltpu.VMEM((NZ, heads, rows, rows), F32),
            pltpu.VMEM(one, F32),
            pltpu.VMEM(one, F32),
            pltpu.VMEM(one, F32),
            pltpu.VMEM(one, F32),
            pltpu.VMEM(one, F32),
            pltpu.VMEM((2, 4, 2, *one), BF16),
            pltpu.VMEM((2, 4, 2, *one), BF16),
            pltpu.VMEM((4, NQ, rows, width), BF16),
            pltpu.VMEM((rows, 3 * width), BF16),
            pltpu.VMEM((NQ, NZ, own, rows), BF16),
            pltpu.VMEM((NQ, NZ, own, rows), BF16),
            pltpu.VMEM((NZ, NQ, own, rows), BF16),
            pltpu.VMEM((NZ, NQ, own, rows), BF16),
            pltpu.VMEM((2, 2, NZ * NQ, own, width), BF16),
            pltpu.VMEM((NT, rows, width), BF16),
            pltpu.VMEM((NT, rows, width), F32),
            pltpu.VMEM((2, rows, HD), F32),
            pltpu.VMEM((2, 4, 4, own, width), BF16),
            pltpu.VMEM((2, 4, 4, own, width), BF16),
            pltpu.VMEM((NZ, 4, own, width), F32),
            pltpu.VMEM((2, 2, 2, rows, width), BF16),
            pltpu.VMEM((2, 2, 2, rows, width), BF16),
            pltpu.VMEM((rows, width), BF16),
            pltpu.VMEM((rows, width), BF16),
            pltpu.VMEM((NT, 16, rows), F32),
            dma((2, 4, 2)),
            dma((2, 4, 2)),
            dma((2, 4, 2)),
            dma((2, 4, 2)),
            dma((3, 2)),
            dma((3, 2)),
            dma((4, 3)),
            dma((4, 3)),
            dma((2, 4, 4)),
            dma((2, 4, 4)),
            dma((2, 2, 2)),
            dma((2, 2, 2)),
            dma,
            dma,
            dma((NT - 1,)),
            dma((NT - 1,)),
            dma((2, 2, 4)),
            dma((2, 2, 4)),
            dma((2, 2, 2, 4)),
            dma((2, 2, 2, 4)),
            dma((2, 9)),
            dma((2, 9)),
            dma((2,)),
            dma((2,)),
            dma((2, 2, 9)),
            dma((2, 2, 9)),
            dma((2, 2, 8)),
            dma((2, 2, 8)),
            dma((4,)),
            dma((NZ,)),
            dma((NZ, heads)),
        ],
        compiler_params=pltpu.CompilerParams(
            collective_id=0, has_side_effects=True, vmem_limit_bytes=67_043_328
        ),
    )(tokens, cot, own_qkv, own_out)


def finish(*arrays):
    def kernel(*refs):
        for i in range(len(arrays)):
            refs[len(arrays) + i][...] = refs[i][...]

    vmem = pl.BlockSpec(memory_space=pltpu.VMEM)
    return pl.pallas_call(
        kernel,
        out_shape=tuple(jax.ShapeDtypeStruct(a.shape, a.dtype) for a in arrays),
        in_specs=[vmem] * len(arrays),
        out_specs=(vmem,) * len(arrays),
    )(*arrays)


def local(tokens, cotangent, qkv_weight, out_weight):
    qkv_grad, out_grad, branch = finish(
        *layer(tokens[0], cotangent[0], jnp.transpose(qkv_weight, (1, 0, 2)), out_weight)
    )
    return (jnp.transpose(qkv_grad, (1, 0, 2)), out_grad, branch[None])


def solution(mesh):
    return jax.shard_map(
        local,
        mesh=mesh,
        in_specs=(
            P("dp", "seq", None),
            P("dp", "seq", None),
            P(("seq", "dp"), None, "tensor"),
            P(("seq", "dp"), "tensor"),
        ),
        out_specs=(
            P(("seq", "dp"), None, "tensor"),
            P(("seq", "dp"), "tensor"),
            P("dp", "seq", "tensor"),
        ),
        check_vma=False,
    )
```

time: 230 us -> 161 us (0.70)
  waiting for transfers between devices: 68.4 us -> 0 us
  Pallas kernels: 118 us -> 160 us
  between operations: 14.1 us -> 0.64 us
  local copies, waits for them, and re-layouts: 12.9 us -> 0 us
  matrix products: 10.4 us -> 0 us
  other arithmetic: 5.65 us -> 0 us
    all_gather x1 -> x0, waiting for transfers between devices: 68.3 us -> none  [local(): weights = lax.all_gather(both, ('seq', 'dp'), axis=0, tiled=True)]
    pallas_call x1, Pallas kernels: 118 us -> 158 us  [layer(): pl.pallas_call(lambda *refs: layer_kernel(heads, *refs), out_shape=(jax.S...]
    dot_general x2 -> x0, matrix products: 10.4 us -> none  [dot(): return lax.dot_general(a, b, dims, preferred_element_type=F32)]
    transpose x2 -> x0, local copies, waits for them, and re-layouts: 4.18 us -> none  [the longest x1 2.6 us: local(): cot_t = grad_rows.T.reshape(NZ, NQ, own, rows)]
    slice x1 -> x0, local copies, waits for them, and re-layouts: 3.45 us -> none  [local(): full_qkv, full_out = (weights[:, :3 * width], weights[:, 3 * width:])]
    transpose x1 -> x0, other arithmetic: 2.37 us -> none  [local(): unit_t = unit_low.T.reshape(NZ, NQ, own, rows)]
  transfers between devices with their start and end apart: 1 -> 0, of which waited for: 1 -> 0; matrix products, arithmetic and copies ran while one was open for 3% -> 0% of each run, Pallas kernels for 0% -> 0%
where the time goes in v4:
time: 161 us; the launch traced here: 160 us
  Pallas kernels  160 us (99%)
    pallas_call x1, Pallas kernels, layer(): pl.pallas_call(lambda *refs: layer_kernel(heads, *refs), out_shape=(jax.S...  158 us

profile of v4, /device:TPU:2, one launch (start us, length us, event | category | flops | bytes accessed | tf_op | source)
XLA Modules:
  0.0 160.2 jit_solution(11123561594573762927)
XLA Ops:
  0.6 157.6 %shard_map.67 = (f32[3,96,384]{2,1,0:T(8,128)}, f32[96,384]{1,0:T(8,128)}, bf16[256,384]{1,0:T(8,128)(2,1)}) custom-call(bf16[256,3072]{1,0:T(8,128)(2,1)} %bitcast.5, bf16[256,3072]{1,0:T(8,128)(2,1)} %bitcast.6, bf16[3,96,384]{2,1,0:T(8,128)(2,1)} %bitcast.7, bf16[96,384]{1,0:T(8,128)(2,1)} %refs_3_.1), custom_call_target="tpu_custom_call" | custom-call | tf_op jit(solution)/shard_map/pallas_call | solution.py:784
  158.2 2.0 %shard_map.68 = (f32[3,96,384]{2,1,0:T(8,128)}, f32[96,384]{1,0:T(8,128)}, bf16[256,384]{1,0:T(8,128)(2,1)}) custom-call(f32[3,96,384]{2,1,0:T(8,128)} %get-tuple-element.9.refs_0_, f32[96,384]{1,0:T(8,128)} %get-tuple-element.10.refs_1_, bf16[256,384]{1,0:T(8,128)(2,1)} %get-tuple-element.11.refs_2_), custom_call_target="tpu_custom_call" | custom-call | tf_op jit(solution)/shard_map/pallas_call | solution.py:870

commit v5 on v4

--- a/solution.py
+++ b/solution.py
@@ -90,18 +90,12 @@
     recv_y,
     send_st,
     recv_st,
-    send_za,
+    send_w,
     recv_za,
-    send_zb,
     recv_zb,
-    send_ya,
     recv_ya,
-    send_yb,
     recv_yb,
-    send_da,
-    recv_da,
-    send_db,
-    recv_db,
+    recv_d,
     load_g,
     load_t,
     load_c,
@@ -118,6 +112,7 @@
     scale = HD ** (-0.5)
     width = heads * HD
     features = NT * width
+    half_block = tokens.shape[0] // 2
 
     barrier = pltpu.get_barrier_semaphore()
     for side in sides:
@@ -144,16 +139,17 @@
         return remote(
             kv.at[b, j],
             kv.at[b, j],
-            send_ag.at[way, step, j],
+            send_ag,
             recv_ag.at[way, step, j],
             {"seq": sides[way]},
         )
 
     def scatter(way, step, j):
+        part_of = pl.ds(way * half_block, half_block) if step == 0 else pl.ds(0, 2 * half_block)
         return remote(
-            sbuf.at[way, step, j],
-            rbuf.at[way, step, j],
-            send_rs.at[way, step, j],
+            sbuf.at[way, step, j, :, part_of],
+            rbuf.at[way, step, j, :, part_of],
+            send_rs,
             recv_rs.at[way, step, j],
             {"seq": sides[way]},
         )
@@ -162,7 +158,7 @@
         return remote(
             sdw.at[way, step, group],
             rdw.at[way, step, group],
-            send_dw.at[way, step, group],
+            send_dw,
             recv_dw.at[way, step, group],
             {"seq": sides[way]},
         )
@@ -172,8 +168,8 @@
         return remote(
             src.at[:, mates[k]],
             dst.at[quad],
-            send_tr.at[k, which],
-            recv_tr.at[k, which],
+            send_tr.at[which],
+            recv_tr.at[which],
             {"dp": mates[k]},
         )
 
@@ -182,7 +178,7 @@
         return remote(
             block,
             block,
-            send_act.at[group, k],
+            send_act,
             recv_act.at[group, k],
             {"dp": mates[1] if k == 1 else mates[0]},
         )
@@ -191,7 +187,7 @@
         return remote(
             xs.at[way, step, half],
             xr.at[way, step, half],
-            send_x.at[way, step, half],
+            send_x,
             recv_x.at[way, step, half],
             {"tensor": xsides[way]},
         )
@@ -203,8 +199,8 @@
         return remote(
             stats.at[0],
             stats.at[k],
-            send_st.at[k - 1],
-            recv_st.at[k - 1],
+            send_st,
+            recv_st,
             {"tensor": lax.rem(part + k, NT)},
         )
 
@@ -213,20 +209,20 @@
 
     mine = me * NQ + quad
     load_own = [
-        pltpu.make_async_copy(own_qkv.at[1], g.at[0, 0, mine], load_g.at[0]),
-        pltpu.make_async_copy(own_qkv.at[2], g.at[0, 1, mine], load_g.at[1]),
-        pltpu.make_async_copy(own_qkv.at[0], g.at[1, 0, mine], load_g.at[2]),
-        pltpu.make_async_copy(own_out, g.at[1, 1, mine], load_g.at[3]),
+        pltpu.make_async_copy(own_qkv.at[1], g.at[0, 0, mine], load_g),
+        pltpu.make_async_copy(own_qkv.at[2], g.at[0, 1, mine], load_g),
+        pltpu.make_async_copy(own_qkv.at[0], g.at[1, 0, mine], load_g),
+        pltpu.make_async_copy(own_out, g.at[1, 1, mine], load_g),
     ]
     load_tokens = [
-        pltpu.make_async_copy(tokens.at[:, z * width : (z + 1) * width], tb.at[z], load_t.at[z])
+        pltpu.make_async_copy(tokens.at[:, z * width : (z + 1) * width], tb.at[z], load_t)
         for z in range(NZ)
     ]
     load_cot = [
         pltpu.make_async_copy(
             cot.at[:, (z * heads + h) * HD : (z * heads + h + 1) * HD],
             sbuf.at[z // 4, z % 4, 1, h],
-            load_c.at[z, h],
+            load_c,
         )
         for z in range(NZ)
         for h in range(heads)
@@ -253,6 +249,9 @@
 
     def second_array(p, i, who):
         return g.at[p, 1, place(i) * NQ + classes[who]]
+
+    def stage(i):
+        return 4 if i >= 7 else (i + 1) // 2
 
     def index(way, step):
         return 0 if step == 0 else 1 + 2 * (step - 1) + way
@@ -270,7 +269,7 @@
                 lax.rem(me + (NZ - step if way == 0 else step), NZ) * NQ + quad,
                 way * half_rows : (way + 1) * half_rows,
             ],
-            send_za.at[p, way, step],
+            send_w,
             recv_za.at[p, way, step],
             {"seq": sides[way]},
         )
@@ -279,52 +278,66 @@
         z = lax.rem(me + (NZ - step if way == 0 else step), NZ)
         return same(
             g.at[p, 1, z * NQ + classes[who]],
-            send_zb.at[p, who, way, step],
+            send_w,
             recv_zb.at[p, who, way, step],
             {"seq": sides[way]},
         )
 
     def ya(p, i):
         return same(
-            first_array(p, i, 0), send_ya.at[p, i], recv_ya.at[p, i], {"dp": mates[1]}
+            first_array(p, i, 0), send_w, recv_ya.at[p, stage(i)], {"dp": mates[1]}
         )
 
     def yb(p):
-        return same(second_array(p, 0, 0), send_yb.at[p], recv_yb.at[p], {"dp": mates[1]})
+        return same(second_array(p, 0, 0), send_w, recv_yb.at[p], {"dp": mates[1]})
 
     def da(p, who, i):
         return same(
             first_array(p, i, who),
-            send_da.at[p, who, i],
-            recv_da.at[p, who, i],
+            send_w,
+            recv_d.at[p, stage(i)],
             {"dp": mates[0]},
         )
 
     def db(p, who, i):
         return same(
             second_array(p, i, who),
-            send_db.at[p, who, i],
-            recv_db.at[p, who, i],
+            send_w,
+            recv_d.at[p, stage(i)],
             {"dp": mates[0]},
         )
 
-    for c in load_own:
-        c.wait()
+    def whole(ref, sem):
+        return pltpu.make_async_copy(ref, ref, sem)
+
+    def units(n):
+        return g.at[0, 0, 0:n]
+
+    def all_sent(ref, sem):
+        remote(ref, ref, sem, sem, {"seq": sides[0]}).wait_send()
+
+    def all_here(ref, sem):
+        remote(ref, ref, sem, sem, {"seq": sides[0]}).wait_recv()
+
+    whole(units(4), load_g).wait()
     pl.semaphore_wait(barrier, 2 + 3 + NT - 1)
+    for way in range(2):
+        za(0, way, 0).start()
     for p in range(2):
-        for way in range(2):
-            za(p, way, 0).start()
         yb(p).start()
+    for way in range(2):
+        zb(0, 0, way, 0).start()
+    for p in range(2):
         ya(p, 0).start()
-        for way in range(2):
-            zb(p, 0, way, 0).start()
+    for way in range(2):
+        za(1, way, 0).start()
+    for p in range(2):
         da(p, 0, 0).start()
         db(p, 0, 0).start()
 
     rows = tb.shape[1]
     blank = jnp.zeros((rows, HD), F32)
-    for c in load_tokens:
-        c.wait()
+    whole(tb, load_t).wait()
 
     def fold(a):
         s = a[:, :HD]
@@ -347,11 +360,10 @@
     norm[0] = average
     norm[1] = lax.rsqrt(lane_sum(lax.fori_loop(0, NZ, add_square, blank)) / features + epsilon)
 
-    for p in range(2):
-        yb(p).wait_recv()
-        for way in range(2):
-            zb(p, 1, way, 0).start()
-        db(p, 1, 0).start()
+    yb(0).wait_recv()
+    for way in range(2):
+        zb(0, 1, way, 0).start()
+    db(0, 1, 0).start()
 
     def lower(z, c):
         for h in range(heads):
@@ -362,8 +374,7 @@
     lax.fori_loop(0, NZ, lower, 0)
     for i in range(4):
         nb[i] = jnp.zeros_like(nb[i])
-    for c in load_cot:
-        c.wait()
+    whole(sbuf.at[:, :, 1], load_c).wait()
 
     def low_rows(z, which):
         return jnp.concatenate(
@@ -396,16 +407,6 @@
                 return c
 
             lax.fori_loop(0, 2, step, 0)
-
-    def other_core(p, i):
-        for who in range(2):
-            da(p, who, i).wait_recv()
-            if i < 8:
-                db(p, who, i).wait_recv()
-
-    def next_chip(p, i):
-        ya(p, i).wait_recv()
-        da(p, 1, i).start()
 
     def ring_step(p, step):
         for way in range(2):
@@ -432,10 +433,10 @@
 
     def settle(p, step):
         these = (0,) if step == 0 else (2 * step - 1, 2 * step) if step < 4 else (7, 8)
+        all_here(units(2 if 0 < step < 4 else 1), recv_ya.at[p, step])
         for i in these:
-            next_chip(p, i)
-        for i in these:
-            other_core(p, i)
+            da(p, 1, i).start()
+        all_here(units(8 if 0 < step < 4 else 4), recv_d.at[p, step])
         products(p, these[0])
 
     def normal(a, j, h):
@@ -448,30 +449,35 @@
 
     ring_step(0, 0)
     turn(0, 2)
+    yb(1).wait_recv()
+    db(1, 1, 0).start()
     settle(0, 0)
     ring_step(0, 1)
+    for who in range(2):
+        for way in range(2):
+            zb(1, who, way, 0).start()
+    turn(2, 2)
     settle(0, 1)
-    turn(2, 2)
-    ring_step(1, 0)
     ring_step(0, 2)
     settle(0, 2)
+    ring_step(1, 0)
+    ring_last(0)
     turn(4, 2)
+    settle(1, 0)
+    settle(0, 3)
     ring_step(1, 1)
-    settle(1, 0)
-    ring_last(0)
-    settle(0, 3)
-    ring_step(1, 2)
     settle(0, 4)
     for h in range(heads):
         at = slice(h * HD, (h + 1) * HD)
         kv[me, 0, h] = normal(nb[0, :, at], 1, h)
         kv[me, 1, h] = nb[1, :, at].astype(BF16)
+    ring_step(1, 2)
     for j in range(2):
         for way in range(2):
             gather(way, 0, j).start()
     settle(1, 1)
+    turn(6, 2)
     settle(1, 2)
-    turn(6, 2)
     ring_last(1)
     for which in range(2):
         for k in range(3):
@@ -544,17 +550,18 @@
     def scatter_step(step):
         for j in range(2):
             for way in range(2):
-                if not goes(way, 3 - step, j):
-                    continue
                 b = lax.rem(me + (4 - step if way == 0 else 4 + step), NZ)
-                added = step > 0 and goes(way, 4 - step, j)
-                if added:
+                if step > 0:
                     scatter(way, step - 1, j).wait_recv()
                 for h in range(heads):
-                    val = ex[b, h, :, j * HD : (j + 1) * HD]
-                    if added:
-                        val = val + rbuf[way, step - 1, j, h].astype(F32)
-                    sbuf[way, step, j, h] = val.astype(BF16)
+                    for r in range(2):
+                        if step == 0 and r != way:
+                            continue
+                        at = slice(r * half_block, (r + 1) * half_block)
+                        val = ex[b, h, at, j * HD : (j + 1) * HD]
+                        if step > 1 or step == 1 and r == way:
+                            val = val + rbuf[way, step - 1, j, h, at].astype(F32)
+                        sbuf[way, step, j, h, at] = val.astype(BF16)
                 scatter(way, step, j).start()
 
     def relay(group):
@@ -567,47 +574,45 @@
 
     backward_blocks(0, 1)
     scatter_step(0)
-    backward_blocks(1, 7)
+    backward_blocks(1, 2)
+    scatter_step(1)
+    backward_blocks(3, 5)
     for h in range(heads):
         a = back(dq[h], 0, h).astype(BF16)
         act[1, quad, :, h * HD : (h + 1) * HD] = a
         low[:, h * HD : (h + 1) * HD] = a
     shared(1, 1).start()
     shared(1, 0).start()
-    scatter_step(1)
     relay(0)
     scatter_step(2)
     relay(1)
     scatter_step(3)
 
-    for which in range(2):
-        for k in range(3):
-            transposed(k, which).wait_recv()
+    for which, there in enumerate((ut, ct)):
+        all_here(there.at[0 : NQ - 1], recv_tr.at[which])
     for group in range(2):
         shared(group, 0).wait_recv()
         shared(group, 2).wait_recv()
 
-    def weight_block(z, group):
+    def weight_blocks(group):
         left = ct if group == 0 else ut
-        acc = dot(left[0, z], act[group, 0])
-        for m in range(1, NQ):
-            acc = acc + dot(left[m, z], act[group, m])
-        dwp[z, group] = acc
-
-    def weight_blocks(*groups):
-        def step(i, c):
-            for group in groups:
-                weight_block(lax.rem(me + 5 + i, NZ), group)
-            return c
-
-        lax.fori_loop(0, NZ - 1, step, 0)
+        tall = (left.shape[1] * left.shape[2], left.shape[3])
+        for m in range(NQ):
+            val = dot(left[m].reshape(tall), act[group, m])
+            if m:
+                val = val + dwp[group]
+            dwp[group] = val
+
+    own_rows = own_out.shape[0]
+
+    def weight_part(z, group):
+        return dwp[group, pl.ds(pl.multiple_of(z * own_rows, own_rows), own_rows), :]
 
     def weight_step(step, group):
         for way in range(2):
             if not goes(way, 3 - step, group):
                 continue
-            z = lax.rem(me + (4 - step if way == 0 else 4 + step), NZ)
-            val = dwp[z, group]
+            val = weight_part(lax.rem(me + (4 - step if way == 0 else 4 + step), NZ), group)
             if step > 0 and goes(way, 4 - step, group):
                 weight_ring(way, step - 1, group).wait_recv()
                 val = val + rdw[way, step - 1, group].astype(F32)
@@ -615,9 +620,8 @@
             weight_ring(way, step, group).start()
 
     for group in range(2):
-        weight_block(lax.rem(me + 4, NZ), group)
+        weight_blocks(group)
         weight_step(0, group)
-    weight_blocks(0, 1)
 
     for j in range(2):
         for way in range(2):
@@ -632,8 +636,8 @@
             low[:, (j + 1) * width + h * HD : (j + 1) * width + (h + 1) * HD] = a
         shared(2 + j, 1).start()
         shared(2 + j, 0).start()
-        for group in range(2):
-            weight_step(1 + j, group)
+    for group in range(2):
+        weight_step(1, group)
 
     def inner(n, sums):
         x = lax.rem(xplace + 2 + n // 2, 4)
@@ -673,40 +677,38 @@
         val = piece(xplace, half)
         return val + xr[0, 1, half].astype(F32) + xr[1, 1, half].astype(F32)
 
-    far = lax.rem(me + 4, NZ)
     zero = jnp.zeros((low.shape[0], HD), F32)
     sums = lax.fori_loop(0, 2, inner, (zero, zero))
     inner_step(0)
-    sums = lax.fori_loop(2, 4, inner, sums)
+    sums = lax.fori_loop(2, 6, inner, sums)
     relay(2)
-    sums = lax.fori_loop(4, NT, inner, sums)
-    shared(2, 0).wait_recv()
-    shared(2, 2).wait_recv()
-    weight_block(far, 2)
-    weight_step(0, 2)
+    sums = lax.fori_loop(6, NT, inner, sums)
     for i in range(2):
         stats[0, i * 8 : (i + 1) * 8, :] = jnp.transpose(lane_sum(sums[i]))[:8]
     for k in range(1, NT):
         stat(k).start()
+    shared(2, 0).wait_recv()
+    shared(2, 2).wait_recv()
+    weight_blocks(2)
+    weight_step(0, 2)
     relay(3)
-    weight_blocks(2)
+    inner_step(1)
+    for group in range(2):
+        weight_step(2, group)
+    shared(3, 0).wait_recv()
+    shared(3, 2).wait_recv()
+    weight_blocks(3)
+    weight_step(0, 3)
+    weight_step(1, 2)
+    weight_step(1, 3)
     for group in range(2):
         weight_step(3, group)
-    inner_step(1)
-    weight_step(1, 2)
-    shared(3, 0).wait_recv()
-    shared(3, 2).wait_recv()
-    weight_block(far, 3)
-    weight_step(0, 3)
-    weight_blocks(3)
     weight_step(2, 2)
     ysend[...] = arrived(0).astype(BF16)
     ypair().start()
-    weight_step(1, 3)
+    weight_step(2, 3)
     weight_step(3, 2)
-    weight_step(2, 3)
-    for k in range(1, NT):
-        stat(k).wait_recv()
+    all_here(stats.at[0 : NT - 1], recv_st)
     total = stats[0]
     for k in range(1, NT):
         total = total + stats[k]
@@ -726,7 +728,7 @@
         branch_out[:, at] = (val * norm[1]).astype(BF16)
 
     for group in range(4):
-        val = dwp[me, group]
+        val = weight_part(me, group)
         for way in range(2):
             weight_ring(way, 3, group).wait_recv()
             val = val + rdw[way, 3, group].astype(F32)
@@ -735,42 +737,16 @@
         else:
             qkv_out[group - 1] = val
 
-    for p in range(2):
-        for way in range(2):
-            for step in range(4):
-                za(p, way, step).wait_send()
-                for who in range(2):
-                    if step < 3 or who == way:
-                        zb(p, who, way, step).wait_send()
-        for i in range(9):
-            ya(p, i).wait_send()
-            for who in range(2):
-                da(p, who, i).wait_send()
-                if i < 8:
-                    db(p, who, i).wait_send()
-        yb(p).wait_send()
-    for step in range(4):
-        for j in range(2):
-            for way in range(2):
-                if goes(way, step, j):
-                    gather(way, step, j).wait_send()
-                if goes(way, 3 - step, j):
-                    scatter(way, step, j).wait_send()
-                    weight_ring(way, step, j).wait_send()
-                    weight_ring(way, step, j + 2).wait_send()
-    for which in range(2):
-        for k in range(3):
-            transposed(k, which).wait_send()
-    for group in range(4):
-        for k in range(3):
-            shared(group, k).wait_send()
-    for way in range(2):
-        xring(way, 0, way).wait_send()
-        for half in range(2):
-            xring(way, 1, half).wait_send()
+    all_sent(g.at[:, :, 0 : NZ * NQ - 1], send_w)
+    all_sent(kv.at[0 : NZ - 1], send_ag)
+    all_sent(kv.at[0 : NZ - 1], send_rs)
+    all_sent(units(28), send_dw)
+    for which, here in enumerate((ut, ct)):
+        all_sent(here.at[0 : NQ - 1], send_tr.at[which])
+    all_sent(act.at[0:3], send_act)
+    all_sent(act.at[0:3, 0:2], send_x)
     ypair().wait_send()
-    for k in range(1, NT):
-        stat(k).wait_send()
+    all_sent(stats.at[0 : NT - 1], send_st)
 
 
 def layer(tokens, cot, own_qkv, own_out):
@@ -817,43 +793,37 @@
             pltpu.VMEM((2, rows, HD), F32),
             pltpu.VMEM((2, 4, 4, own, width), BF16),
             pltpu.VMEM((2, 4, 4, own, width), BF16),
-            pltpu.VMEM((NZ, 4, own, width), F32),
+            pltpu.VMEM((4, NZ * own, width), F32),
             pltpu.VMEM((2, 2, 2, rows, width), BF16),
             pltpu.VMEM((2, 2, 2, rows, width), BF16),
             pltpu.VMEM((rows, width), BF16),
             pltpu.VMEM((rows, width), BF16),
             pltpu.VMEM((NT, 16, rows), F32),
+            dma,
             dma((2, 4, 2)),
+            dma,
             dma((2, 4, 2)),
-            dma((2, 4, 2)),
-            dma((2, 4, 2)),
-            dma((3, 2)),
-            dma((3, 2)),
+            dma((2,)),
+            dma((2,)),
+            dma,
             dma((4, 3)),
-            dma((4, 3)),
+            dma,
             dma((2, 4, 4)),
-            dma((2, 4, 4)),
+            dma,
             dma((2, 2, 2)),
-            dma((2, 2, 2)),
-            dma,
-            dma,
-            dma((NT - 1,)),
-            dma((NT - 1,)),
-            dma((2, 2, 4)),
+            dma,
+            dma,
+            dma,
+            dma,
+            dma,
             dma((2, 2, 4)),
             dma((2, 2, 2, 4)),
-            dma((2, 2, 2, 4)),
-            dma((2, 9)),
-            dma((2, 9)),
+            dma((2, 5)),
             dma((2,)),
-            dma((2,)),
-            dma((2, 2, 9)),
-            dma((2, 2, 9)),
-            dma((2, 2, 8)),
-            dma((2, 2, 8)),
-            dma((4,)),
-            dma((NZ,)),
-            dma((NZ, heads)),
+            dma((2, 5)),
+            dma,
+            dma,
+            dma,
         ],
         compiler_params=pltpu.CompilerParams(
             collective_id=0, has_side_effects=True, vmem_limit_bytes=67_043_328

time: 161 us -> 150 us (0.932)
  Pallas kernels: 160 us -> 148 us
    pallas_call x1, Pallas kernels: 158 us -> 146 us  [layer(): pl.pallas_call(lambda *refs: layer_kernel(heads, *refs), out_shape=(jax.S...]
where the time goes in v5:
time: 150 us; the launch traced here: 149 us
  Pallas kernels  148 us (99%)
    pallas_call x1, Pallas kernels, layer(): pl.pallas_call(lambda *refs: layer_kernel(heads, *refs), out_shape=(jax.S...  146 us

profile of v5, /device:TPU:2, one launch (start us, length us, event | category | flops | bytes accessed | tf_op | source)
XLA Modules:
  0.0 148.9 jit_solution(933697086948753059)
XLA Ops:
  0.6 146.2 %shard_map.67 = (f32[3,96,384]{2,1,0:T(8,128)}, f32[96,384]{1,0:T(8,128)}, bf16[256,384]{1,0:T(8,128)(2,1)}) custom-call(bf16[256,3072]{1,0:T(8,128)(2,1)} %bitcast.5, bf16[256,3072]{1,0:T(8,128)(2,1)} %bitcast.6, bf16[3,96,384]{2,1,0:T(8,128)(2,1)} %bitcast.7, bf16[96,384]{1,0:T(8,128)(2,1)} %refs_3_.1), custom_call_target="tpu_custom_call" | custom-call | tf_op jit(solution)/shard_map/pallas_call | solution.py:760
  146.9 2.0 %shard_map.68 = (f32[3,96,384]{2,1,0:T(8,128)}, f32[96,384]{1,0:T(8,128)}, bf16[256,384]{1,0:T(8,128)(2,1)}) custom-call(f32[3,96,384]{2,1,0:T(8,128)} %get-tuple-element.9.refs_0_, f32[96,384]{1,0:T(8,128)} %get-tuple-element.10.refs_1_, bf16[256,384]{1,0:T(8,128)(2,1)} %get-tuple-element.11.refs_2_), custom_call_target="tpu_custom_call" | custom-call | tf_op jit(solution)/shard_map/pallas_call | solution.py:840

commit v6 on v5

--- a/solution.py
+++ b/solution.py
@@ -464,17 +464,18 @@
     ring_last(0)
     turn(4, 2)
     settle(1, 0)
+    ring_step(1, 1)
     settle(0, 3)
-    ring_step(1, 1)
     settle(0, 4)
     for h in range(heads):
         at = slice(h * HD, (h + 1) * HD)
         kv[me, 0, h] = normal(nb[0, :, at], 1, h)
         kv[me, 1, h] = nb[1, :, at].astype(BF16)
+    for way in range(2):
+        gather(way, 0, 0).start()
     ring_step(1, 2)
-    for j in range(2):
-        for way in range(2):
-            gather(way, 0, j).start()
+    for way in range(2):
+        gather(way, 0, 1).start()
     settle(1, 1)
     turn(6, 2)
     settle(1, 2)
@@ -482,6 +483,9 @@
     for which in range(2):
         for k in range(3):
             transposed(k, which).start()
+    for way in range(2):
+        gather(way, 0, 0).wait_recv()
+        gather(way, 1, 0).start()
     settle(1, 3)
     settle(1, 4)
     for h in range(heads):
@@ -513,6 +517,8 @@
     for step in range(3):
         for j in range(2):
             for way in range(2):
+                if step == 0 and j == 0:
+                    continue
                 gather(way, step, j).wait_recv()
                 if goes(way, step + 1, j):
                     gather(way, step + 1, j).start()
@@ -586,7 +592,6 @@
     relay(0)
     scatter_step(2)
     relay(1)
-    scatter_step(3)
 
     for which, there in enumerate((ut, ct)):
         all_here(there.at[0 : NQ - 1], recv_tr.at[which])
@@ -619,9 +624,35 @@
             sdw[way, step, group] = val.astype(BF16)
             weight_ring(way, step, group).start()
 
+    def early_ring(way, step):
+        both = slice(0, 2)
+        return remote(
+            sdw.at[way, step, both],
+            rdw.at[way, step, both],
+            send_dw,
+            recv_dw.at[way, step, 0],
+            {"seq": sides[way]},
+        )
+
+    def early_step(step):
+        for way in range(2):
+            if step == 1:
+                weight_ring(way, 0, way).wait_recv()
+            else:
+                early_ring(way, step - 1).wait_recv()
+            z = lax.rem(me + (4 - step if way == 0 else 4 + step), NZ)
+            for group in range(2):
+                val = weight_part(z, group)
+                if step > 1 or group == way:
+                    val = val + rdw[way, step - 1, group].astype(F32)
+                sdw[way, step, group] = val.astype(BF16)
+            early_ring(way, step).start()
+
     for group in range(2):
         weight_blocks(group)
         weight_step(0, group)
+    scatter_step(3)
+    early_step(1)
 
     for j in range(2):
         for way in range(2):
@@ -636,8 +667,6 @@
             low[:, (j + 1) * width + h * HD : (j + 1) * width + (h + 1) * HD] = a
         shared(2 + j, 1).start()
         shared(2 + j, 0).start()
-    for group in range(2):
-        weight_step(1, group)
 
     def inner(n, sums):
         x = lax.rem(xplace + 2 + n // 2, 4)
@@ -680,29 +709,28 @@
     zero = jnp.zeros((low.shape[0], HD), F32)
     sums = lax.fori_loop(0, 2, inner, (zero, zero))
     inner_step(0)
-    sums = lax.fori_loop(2, 6, inner, sums)
     relay(2)
+    early_step(2)
+    sums = lax.fori_loop(2, 4, inner, sums)
+    shared(2, 0).wait_recv()
+    shared(2, 2).wait_recv()
+    weight_blocks(2)
+    weight_step(0, 2)
+    sums = lax.fori_loop(4, 6, inner, sums)
+    relay(3)
     sums = lax.fori_loop(6, NT, inner, sums)
     for i in range(2):
         stats[0, i * 8 : (i + 1) * 8, :] = jnp.transpose(lane_sum(sums[i]))[:8]
     for k in range(1, NT):
         stat(k).start()
-    shared(2, 0).wait_recv()
-    shared(2, 2).wait_recv()
-    weight_blocks(2)
-    weight_step(0, 2)
-    relay(3)
     inner_step(1)
-    for group in range(2):
-        weight_step(2, group)
     shared(3, 0).wait_recv()
     shared(3, 2).wait_recv()
     weight_blocks(3)
     weight_step(0, 3)
     weight_step(1, 2)
+    early_step(3)
     weight_step(1, 3)
-    for group in range(2):
-        weight_step(3, group)
     weight_step(2, 2)
     ysend[...] = arrived(0).astype(BF16)
     ypair().start()
@@ -730,7 +758,10 @@
     for group in range(4):
         val = weight_part(me, group)
         for way in range(2):
-            weight_ring(way, 3, group).wait_recv()
+            if group > 1:
+                weight_ring(way, 3, group).wait_recv()
+            elif group == 0:
+                early_ring(way, 3).wait_recv()
             val = val + rdw[way, 3, group].astype(F32)
         if group == 0:
             out_out[...] = val

time: 150 us -> 145 us (0.967)
  Pallas kernels: 148 us -> 144 us
    pallas_call x1, Pallas kernels: 146 us -> 142 us  [layer(): pl.pallas_call(lambda *refs: layer_kernel(heads, *refs), out_shape=(jax.S...]
where the time goes in v6:
time: 145 us
  Pallas kernels  144 us (99%)
    pallas_call x1, Pallas kernels, layer(): pl.pallas_call(lambda *refs: layer_kernel(heads, *refs), out_shape=(jax.S...  142 us

profile of v6, /device:TPU:2, one launch (start us, length us, event | category | flops | bytes accessed | tf_op | source)
XLA Modules:
  0.0 144.5 jit_solution(10702225757268445221)
XLA Ops:
  0.6 141.9 %shard_map.67 = (f32[3,96,384]{2,1,0:T(8,128)}, f32[96,384]{1,0:T(8,128)}, bf16[256,384]{1,0:T(8,128)(2,1)}) custom-call(bf16[256,3072]{1,0:T(8,128)(2,1)} %bitcast.5, bf16[256,3072]{1,0:T(8,128)(2,1)} %bitcast.6, bf16[3,96,384]{2,1,0:T(8,128)(2,1)} %bitcast.7, bf16[96,384]{1,0:T(8,128)(2,1)} %refs_3_.1), custom_call_target="tpu_custom_call" | custom-call | tf_op jit(solution)/shard_map/pallas_call | solution.py:791
  142.5 2.0 %shard_map.68 = (f32[3,96,384]{2,1,0:T(8,128)}, f32[96,384]{1,0:T(8,128)}, bf16[256,384]{1,0:T(8,128)(2,1)}) custom-call(f32[3,96,384]{2,1,0:T(8,128)} %get-tuple-element.9.refs_0_, f32[96,384]{1,0:T(8,128)} %get-tuple-element.10.refs_1_, bf16[256,384]{1,0:T(8,128)(2,1)} %get-tuple-element.11.refs_2_), custom_call_target="tpu_custom_call" | custom-call | tf_op jit(solution)/shard_map/pallas_call | solution.py:871

commit v7 on v6

--- a/solution.py
+++ b/solution.py
@@ -431,13 +431,17 @@
             zb(p, way, way, 3).wait_recv()
             db(p, way, 7).start()
 
+    def arrivals(step):
+        return (0,) if step == 0 else (2 * step - 1, 2 * step) if step < 4 else (7, 8)
+
+    def lift(p, step):
+        all_here(units(2 if 0 < step < 4 else 1), recv_ya.at[p, step])
+        for i in arrivals(step):
+            da(p, 1, i).start()
+
     def settle(p, step):
-        these = (0,) if step == 0 else (2 * step - 1, 2 * step) if step < 4 else (7, 8)
-        all_here(units(2 if 0 < step < 4 else 1), recv_ya.at[p, step])
-        for i in these:
-            da(p, 1, i).start()
         all_here(units(8 if 0 < step < 4 else 4), recv_d.at[p, step])
-        products(p, these[0])
+        products(p, arrivals(step)[0])
 
     def normal(a, j, h):
         c = a - lane_mean(a)
@@ -451,21 +455,27 @@
     turn(0, 2)
     yb(1).wait_recv()
     db(1, 1, 0).start()
-    settle(0, 0)
+    lift(0, 0)
     ring_step(0, 1)
     for who in range(2):
         for way in range(2):
             zb(1, who, way, 0).start()
     turn(2, 2)
+    lift(0, 1)
+    settle(0, 0)
+    ring_step(0, 2)
+    lift(0, 2)
     settle(0, 1)
-    ring_step(0, 2)
-    settle(0, 2)
     ring_step(1, 0)
     ring_last(0)
     turn(4, 2)
+    lift(1, 0)
+    lift(0, 3)
+    settle(0, 2)
+    ring_step(1, 1)
+    lift(0, 4)
+    settle(0, 3)
     settle(1, 0)
-    ring_step(1, 1)
-    settle(0, 3)
     settle(0, 4)
     for h in range(heads):
         at = slice(h * HD, (h + 1) * HD)
@@ -476,6 +486,8 @@
     ring_step(1, 2)
     for way in range(2):
         gather(way, 0, 1).start()
+    lift(1, 1)
+    lift(1, 2)
     settle(1, 1)
     turn(6, 2)
     settle(1, 2)
@@ -486,8 +498,13 @@
     for way in range(2):
         gather(way, 0, 0).wait_recv()
         gather(way, 1, 0).start()
+    lift(1, 3)
     settle(1, 3)
+    lift(1, 4)
     settle(1, 4)
+    for way in range(2):
+        gather(way, 0, 1).wait_recv()
+        gather(way, 1, 1).start()
     for h in range(heads):
         at = slice(h * HD, (h + 1) * HD)
         q_low[h] = normal(nb[2, :, at], 0, h)
@@ -517,7 +534,7 @@
     for step in range(3):
         for j in range(2):
             for way in range(2):
-                if step == 0 and j == 0:
+                if step == 0:
                     continue
                 gather(way, step, j).wait_recv()
                 if goes(way, step + 1, j):
@@ -729,9 +746,9 @@
     weight_blocks(3)
     weight_step(0, 3)
     weight_step(1, 2)
-    early_step(3)
     weight_step(1, 3)
     weight_step(2, 2)
+    early_step(3)
     ysend[...] = arrived(0).astype(BF16)
     ypair().start()
     weight_step(2, 3)

time: 145 us -> 145 us (level); the launches traced: 145 us -> 143 us
  Pallas kernels: 144 us -> 142 us
    pallas_call x1, Pallas kernels: 142 us -> 140 us  [layer(): pl.pallas_call(lambda *refs: layer_kernel(heads, *refs), out_shape=(jax.S...]
where the time goes in v7:
time: 145 us; the launch traced here: 143 us
  Pallas kernels  142 us (98%)
    pallas_call x1, Pallas kernels, layer(): pl.pallas_call(lambda *refs: layer_kernel(heads, *refs), out_shape=(jax.S...  140 us

profile of v7, /device:TPU:2, one launch (start us, length us, event | category | flops | bytes accessed | tf_op | source)
XLA Modules:
  0.0 142.6 jit_solution(14494237794885831301)
XLA Ops:
  0.6 140.0 %shard_map.67 = (f32[3,96,384]{2,1,0:T(8,128)}, f32[96,384]{1,0:T(8,128)}, bf16[256,384]{1,0:T(8,128)(2,1)}) custom-call(bf16[256,3072]{1,0:T(8,128)(2,1)} %bitcast.5, bf16[256,3072]{1,0:T(8,128)(2,1)} %bitcast.6, bf16[3,96,384]{2,1,0:T(8,128)(2,1)} %bitcast.7, bf16[96,384]{1,0:T(8,128)(2,1)} %refs_3_.1), custom_call_target="tpu_custom_call" | custom-call | tf_op jit(solution)/shard_map/pallas_call | solution.py:808
  140.6 2.0 %shard_map.68 = (f32[3,96,384]{2,1,0:T(8,128)}, f32[96,384]{1,0:T(8,128)}, bf16[256,384]{1,0:T(8,128)(2,1)}) custom-call(f32[3,96,384]{2,1,0:T(8,128)} %get-tuple-element.9.refs_0_, f32[96,384]{1,0:T(8,128)} %get-tuple-element.10.refs_1_, bf16[256,384]{1,0:T(8,128)(2,1)} %get-tuple-element.11.refs_2_), custom_call_target="tpu_custom_call" | custom-call | tf_op jit(solution)/shard_map/pallas_call | solution.py:888

commit v8 on v7

--- a/solution.py
+++ b/solution.py
@@ -329,8 +329,6 @@
         zb(0, 0, way, 0).start()
     for p in range(2):
         ya(p, 0).start()
-    for way in range(2):
-        za(1, way, 0).start()
     for p in range(2):
         da(p, 0, 0).start()
         db(p, 0, 0).start()
@@ -452,6 +450,8 @@
         return u.astype(BF16)
 
     ring_step(0, 0)
+    for way in range(2):
+        za(1, way, 0).start()
     turn(0, 2)
     yb(1).wait_recv()
     db(1, 1, 0).start()

time: 145 us -> 146 us (level)
  no operation moved by 1% of the time
where the time goes in v8:
time: 146 us; the launch traced here: 144 us
  Pallas kernels  143 us (98%)
    pallas_call x1, Pallas kernels, layer(): pl.pallas_call(lambda *refs: layer_kernel(heads, *refs), out_shape=(jax.S...  141 us

profile of v8, /device:TPU:2, one launch (start us, length us, event | category | flops | bytes accessed | tf_op | source)
XLA Modules:
  0.0 143.6 jit_solution(16157835653428733529)
XLA Ops:
  0.6 141.0 %shard_map.67 = (f32[3,96,384]{2,1,0:T(8,128)}, f32[96,384]{1,0:T(8,128)}, bf16[256,384]{1,0:T(8,128)(2,1)}) custom-call(bf16[256,3072]{1,0:T(8,128)(2,1)} %bitcast.5, bf16[256,3072]{1,0:T(8,128)(2,1)} %bitcast.6, bf16[3,96,384]{2,1,0:T(8,128)(2,1)} %bitcast.7, bf16[96,384]{1,0:T(8,128)(2,1)} %refs_3_.1), custom_call_target="tpu_custom_call" | custom-call | tf_op jit(solution)/shard_map/pallas_call | solution.py:808
  141.6 2.0 %shard_map.68 = (f32[3,96,384]{2,1,0:T(8,128)}, f32[96,384]{1,0:T(8,128)}, bf16[256,384]{1,0:T(8,128)(2,1)}) custom-call(f32[3,96,384]{2,1,0:T(8,128)} %get-tuple-element.9.refs_0_, f32[96,384]{1,0:T(8,128)} %get-tuple-element.10.refs_1_, bf16[256,384]{1,0:T(8,128)(2,1)} %get-tuple-element.11.refs_2_), custom_call_target="tpu_custom_call" | custom-call | tf_op jit(solution)/shard_map/pallas_call | solution.py:888
